TPU v7x, 128 devices: a whole 4x4x4 slice. The times are simulated.
128 devices in a mesh: tm: 32 (over z_hi, y, x), freq: 4 (over z_lo, core).
Axes of the slice: x: 4, y: 4, z: 4 (z_hi: 2, z_lo: 2; z = z_hi * 2 + z_lo), core: 2. Of those that a mesh axis runs over, the one named last changes fastest.
Arguments:
- sfts: float32 [1536, 2, 4096], P('tm', None, 'freq'), may hold values from -40 to 40
- detector_ids: int32 [1536], replicated, may hold values from 0 to 2
- intersection: float32 [3, 3], replicated, may hold values from 0.3 to 1
- lags: int32 [12], replicated, may hold values from 1 to 16, as said below
- template_ids: int32 [4096, 2], P('tm'), may hold values from 0 to 63
Outputs:
- stat: float32 [4096, 4096], P('tm', 'freq')
Inputs may be any that keep to these rules, and one draw needn't show every extreme that they name: 12 distinct lags, one of them 16.
All inputs are finite; a program needn't handle non-finite values.
Results may differ from a plain program's by a relative error of at most 0.009.
Values may be sent and summed in bfloat16 or wider, within the bound.
A program may use at most 64 MiB of HBM per device.

v0:
```python
import math

import jax
import jax.numpy as jnp
from jax import lax
from jax.sharding import PartitionSpec as P

NBIN = 4096
LAGMAX = 16
NGRID = 64
PERIOD = 283


def copy_for_each(value, axis):
    copies = jnp.broadcast_to(value, (lax.axis_size(axis), *value.shape))
    return lax.all_to_all(copies, axis, split_axis=0, concat_axis=0, tiled=True)


def over_copies(value, axis):
    return copy_for_each(value, axis).sum(axis=0)


def shifted(block, axis, distance):
    devices = range(lax.axis_size(axis))
    route = [(i - distance, i) for i in devices if i - distance in devices]
    return lax.ppermute(block, axis, route)


def laid_out(tiles, dim):
    lengths = list(tiles.shape[1:])
    lengths[dim] *= tiles.shape[0]
    return jnp.moveaxis(tiles, 0, dim).reshape(lengths)


def collect(value, axis, dim):
    return laid_out(copy_for_each(value, axis), dim)


def block_term(
    extended, first_row, ids_padded, lag_list, intersection, amplitude_idx, phase_idx, total
):
    span = extended.shape[0] - LAGMAX
    here = jnp.arange(span, dtype=jnp.int32)
    partner = here[None, :] + lag_list[:, None]
    own_rows = extended[:span].astype(jnp.float32)
    far_rows = extended[partner].astype(jnp.float32)
    det_block = lax.dynamic_slice_in_dim(ids_padded, first_row, extended.shape[0], 0)
    det_near = det_block[:span]
    det_far = det_block[partner]
    levels = jnp.arange(intersection.shape[0], dtype=jnp.int32)
    hot_near = (det_near[:, None] == levels[None, :]).astype(jnp.float32)
    hot_far = (det_far[:, :, None] == levels[None, None, :]).astype(jnp.float32)
    weight = jnp.einsum("sa,ab,lsb->ls", hot_near, intersection, hot_far)
    inside = first_row + partner < total
    weight = jnp.where(inside, weight, jnp.float32(0.0))
    re_own = own_rows[None, :, 0]
    im_own = own_rows[None, :, 1]
    re_far = far_rows[:, :, 0]
    im_far = far_rows[:, :, 1]
    pair_re = (weight[:, :, None] * (re_own * re_far + im_own * im_far)).astype(jnp.bfloat16)
    pair_im = (weight[:, :, None] * (re_own * im_far - im_own * re_far)).astype(jnp.bfloat16)
    width = extended.shape[2]
    stacked = jnp.concatenate([pair_re.reshape(-1, width), pair_im.reshape(-1, width)], 0)
    position = first_row + jnp.arange(extended.shape[0], dtype=jnp.int32)
    orbit = 2.0 * math.pi / PERIOD * (position % PERIOD).astype(jnp.float32)
    offset = 2.0 * math.pi / NGRID * phase_idx.astype(jnp.float32)
    sine = jnp.sin(offset[:, None] + orbit[None, :])
    amplitude = 8.0 + 4.0 * amplitude_idx.astype(jnp.float32)
    phase = amplitude[:, None, None] * (sine[:, partner] - sine[:, None, :span])
    rows = phase.shape[0]
    factors = jnp.concatenate(
        [
            jnp.cos(phase).reshape(rows, -1).astype(jnp.bfloat16),
            jnp.sin(phase).reshape(rows, -1).astype(jnp.bfloat16),
        ],
        1,
    )
    return jnp.dot(factors, stacked, preferred_element_type=jnp.float32)


def shards(sfts, detector_ids, intersection, lags, template_ids):
    local_power = jnp.sum(sfts[:, 0] * sfts[:, 0] + sfts[:, 1] * sfts[:, 1], axis=1)
    power = over_copies(local_power, "freq") / NBIN
    white = (sfts * lax.rsqrt(power + 1e-06)[:, None, None]).astype(jnp.bfloat16)
    next_rim = shifted(white[:LAGMAX], "tm", -1)
    extended = jnp.concatenate([white, next_rim], 0)
    total = detector_ids.shape[0]
    ids_padded = jnp.pad(detector_ids, (0, LAGMAX))
    scale = jnp.float32(1.0 / math.sqrt(total * lags.shape[0]))
    table = collect(template_ids, "tm", 0)
    first_row = lax.axis_index("tm") * white.shape[0]
    sums = lax.psum_scatter(
        block_term(
            extended, first_row, ids_padded, lags, intersection, table[:, 0], table[:, 1], total
        ),
        "tm",
        scatter_dimension=0,
        tiled=True,
    )
    return sums * scale


def solution(mesh):
    in_specs = (P("tm", None, "freq"), P(), P(), P(), P("tm", None))
    out_specs = P("tm", "freq")
    return jax.shard_map(shards, mesh=mesh, in_specs=in_specs, out_specs=out_specs, check_vma=False)
```

profile of v0, /device:TPU:0, one launch (start us, length us, event | category | flops | bytes accessed | tf_op | source)
XLA Modules:
  0.0 368.6 jit_solution(12446988611074582523)
XLA Ops:
  6.5 1.7 add_reduce_fusion
  8.2 0.6 broadcast_in_dim.9
  8.8 3.3 all-to-all-start.1
  12.1 0.7 compare_select_fusion
  12.8 0.1 reshape.108
  12.9 0.8 pad_dynamic-slice_fusion
  13.7 3.8 %gather_fusion.1 = s32[576]{0:T(1024)S(1)} fusion(s32[64]{0:T(128)S(1)} %pad_dynamic-slice_fusion, s32[1024]{0:T(1024)S(1)} %pad_clamp_fusion), kind=kCustom, calls=%fused_computation.1 | custom fusion | bytes 6912 | tf_op jit(solution)/shard_map/gather | solution.py:49
  17.6 0.2 fusion.14
  17.8 0.3 select_reduce_fusion
  18.2 0.6 broadcast_in_dim.7
  18.9 10.7 %all-to-all-start = ((s32[32,128,2]{1,2,0:T(2,128)}), s32[32,128,2]{1,2,0:T(2,128)S(1)}, u32[]{:S(2)}, u32[]{:S(2)}) async-start(s32[32,128,2]{1,2,0:T(2,128)} %broadcast_in_dim.7), calls=%async_computation | async-start | bytes 65536 | tf_op jit(solution)/shard_map/all_to_all | solution.py:16
  29.6 0.2 multiply_convert_fusion
  29.9 0.3 fusion.23
  30.2 1.3 collective-permute-start
  31.6 7.8 %all-to-all-done = s32[32,128,2]{1,2,0:T(2,128)S(1)} async-done(((s32[32,128,2]{1,2,0:T(2,128)}), s32[32,128,2]{1,2,0:T(2,128)S(1)}, u32[]{:S(2)}, u32[]{:S(2)}) %all-to-all-start) | async-done | bytes 32800 | tf_op jit(solution)/shard_map/all_to_all | solution.py:16
  39.4 3.4 add_sine_fusion
  42.9 6.3 %gather_fusion = f32[576,4096]{1,0:T(8,128)} fusion(f32[4096,64]{0,1:T(8,128)S(1)} %add_sine_fusion, s32[1024]{0:T(1024)S(1)} %pad_clamp_fusion), kind=kCustom, calls=%fused_computation | custom fusion | bytes 18876672 | tf_op jit(solution)/shard_map/gather | solution.py:69
  49.2 5.3 %broadcast_subtract_fusion = f32[4096,12,48]{0,2,1:T(8,128)S(1)} fusion(f32[4096,12,48]{0,2,1:T(8,128)} %bitcast.61, f32[4096,48]{0,1:T(8,128)S(1)} %slice.54), kind=kLoop, calls=%fused_computation.10 | loop fusion | flops 2359296 | bytes 19660800 | tf_op jit(solution)/shard_map/sub | solution.py:69
  54.6 36.4 %cosine_convert_fusion = (bf16[4096,576]{0,1:T(8,128)(2,1)}, bf16[4096,576]{0,1:T(8,128)(2,1)}) fusion(f32[4096,12,48]{0,2,1:T(8,128)S(1)} %broadcast_subtract_fusion, f32[4096]{0:T(1024)S(1)} %bitcast.69), kind=kLoop, calls=%fused_computation.9 | loop fusion | flops 7077888 | bytes 18890752 | tf_op jit(solution)/shard_map/convert_element_type | solution.py:73
  91.0 0.3 pad_maximum_fusion
  91.4 23.3 %gather_fusion.2 = bf16[576,2,1024]{2,1,0:T(2,128)(2,1)S(1)} fusion(bf16[64,2,1024]{2,1,0:T(2,128)(2,1)S(1)} %pad_maximum_fusion, s32[1024]{0:T(1024)S(1)} %pad_clamp_fusion), kind=kCustom, calls=%fused_computation.2 | custom fusion | bytes 4720896 | tf_op jit(solution)/shard_map/gather | solution.py:46
  114.6 4.5 %fusion.22 = (f32[12,48,1,1024]{3,2,1,0:T(1,128)S(1)}, f32[12,48,1,1024]{3,2,1,0:T(1,128)S(1)}) fusion(bf16[12,48,2,1024]{3,2,1,0:T(2,128)(2,1)S(1)} %bitcast.62), kind=kLoop, calls=%fused_computation.52 | loop fusion | bytes 9437184 | tf_op jit(solution)/shard_map/slice | solution.py:58
  119.2 0.5 copy.16
  119.8 0.5 copy.18
  120.3 0.9 fusion.6
  121.2 0.1 slice-done
  121.4 1.3 slice-done.2
  122.7 0.2 slice-done.1
  122.8 0.2 slice-done.3
  123.0 14.0 %fusion = f32[4096,1024]{1,0:T(8,128)} fusion(bf16[4096,576]{0,1:T(8,128)(2,1)S(1)} %bitcast.66, bf16[4096,576]{0,1:T(8,128)(2,1)S(1)} %bitcast.64, bf16[576,1024]{1,0:T(8,128)(2,1)S(1)} %get-tuple-element.8, bf16[576,1024]{1,0:T(8,128)(2,1)S(1)} %get-tuple-element.7), kind=kOutput, calls=%fused_computation.3 | convolution fusion | flops 9687269376 | bytes 28573696 | tf_op jit(solution)/shard_map/dot_general | solution.py:78
  136.9 222.9 %reduce-scatter.2.cloned.1.call-done = f32[128,1024]{1,0:T(8,128)} async-done(((f32[4096,1024]{1,0:T(8,128)}), f32[128,1024]{1,0:T(8,128)}) %reduce-scatter.2.cloned.1.call-update) | async-done | bytes 524304 | tf_op jit(solution)/shard_map/reduce_scatter | solution.py:92
  359.9 1.9 broadcast_multiply_fusion
  (29 shorter events, 0.6 us)
Async XLA Ops:
  6.5 11.0 %copy-start = (f32[3,3]{1,0:T(4,128)S(1)}, f32[3,3]{1,0:T(4,128)}, u32[]{:S(2)}) copy-start(f32[3,3]{1,0:T(4,128)} %param.7) | copy-start | bytes 112
  8.8 9.4 %all-to-all-start.1 = ((f32[4,1,48]{2,1,0:T(1,128)}), f32[4,1,48]{2,1,0:T(1,128)S(1)}, u32[]{:S(2)}, u32[]{:S(2)}) async-start(f32[4,1,48]{2,1,0:T(1,128)} %broadcast_in_dim.9), calls=%async_computation.1 | async-start | bytes 4096 | tf_op jit(solution)/shard_map/all_to_all | solution.py:16
  13.7 4.4 %copy-start.2 = (s32[12]{0:T(128)S(1)}, s32[12]{0:T(128)}, u32[]{:S(2)}) copy-start(s32[12]{0:T(128)} %param.8) | copy-start | bytes 148
  13.7 4.5 %copy-start.3 = (s32[128,2]{0,1:T(2,128)S(1)}, s32[128,2]{0,1:T(2,128)}, u32[]{:S(2)}) copy-start(s32[128,2]{0,1:T(2,128)} %param.9) | copy-start | bytes 3076
  13.7 15.9 %copy-start.1 = (f32[48,2,1024]{2,1,0:T(2,128)S(1)}, f32[48,2,1024]{2,1,0:T(2,128)}, u32[]{:S(2)}) copy-start(f32[48,2,1024]{2,1,0:T(2,128)} %param.5) | copy-start | bytes 1179652
  18.9 20.5 %all-to-all-start = ((s32[32,128,2]{1,2,0:T(2,128)}), s32[32,128,2]{1,2,0:T(2,128)S(1)}, u32[]{:S(2)}, u32[]{:S(2)}) async-start(s32[32,128,2]{1,2,0:T(2,128)} %broadcast_in_dim.7), calls=%async_computation | async-start | bytes 65536 | tf_op jit(solution)/shard_map/all_to_all | solution.py:16
  29.6 330.3 %reduce-scatter.2.cloned.1.call-start = ((), (), s32[]{:S(2)}) async-start(), calls=%async_computation.3 | async-start | bytes 17301504 | tf_op jit(solution)/shard_map/reduce_scatter | solution.py:92
  30.2 60.8 %collective-permute-start = (bf16[16,2,1024]{2,1,0:T(2,128)(2,1)S(1)}, bf16[16,2,1024]{2,1,0:T(2,128)(2,1)S(1)}, u32[]{:S(2)}, u32[]{:S(2)}) collective-permute-start(bf16[16,2,1024]{2,1,0:T(2,128)(2,1)S(1)} %slice.56), channel_id=1, source_target_pairs={{4,0},{8,4},{12,8},{16,12},{20,16},{24,20},{28,24},{32,28},{36,32}... | collective-permute-start | bytes 196616 | tf_op jit(solution)/shard_map/ppermute | solution.py:26
  119.2 2.2 slice-start
  119.2 3.5 slice-start.2
  119.7 3.1 slice-start.1
  119.8 3.2 slice-start.3
Sparse Core Ops, SparseCore 0:
  137.1 222.7 reduce-scatter.1
where the time goes:
time: 369 us
  waiting for transfers between devices  231 us (63%)
  other arithmetic  51.4 us (14%)
  local copies, waits for them, and re-layouts  43.4 us (12%)
  starting transfers between devices  15.3 us (4%)
  matrix products  14.1 us (4%)
  between operations  13.6 us (4%)
    reduce_scatter x1, waiting for transfers between devices, shards(): lax.psum_scatter(block_term(extended, first_row, ids_padded, lags, inters...  223 us
    convert_element_type x1, other arithmetic, block_term(): jnp.cos(phase).reshape(rows, -1).astype(jnp.bfloat16)  36.4 us
    gather x1, local copies, waits for them, and re-layouts, block_term(): far_rows = extended[partner].astype(jnp.float32)  23.3 us
    all_to_all x2, starting transfers between devices, copy_for_each(): return lax.all_to_all(copies, axis, split_axis=0, concat_axis=0, tiled=True)  14 us
    dot_general x1, matrix products, block_term(): return jnp.dot(factors, stacked, preferred_element_type=jnp.float32)  14 us
    all_to_all x2, waiting for transfers between devices, copy_for_each(): return lax.all_to_all(copies, axis, split_axis=0, concat_axis=0, tiled=True)  7.81 us
  transfers between devices with their start and end apart: 4, of which 2 were waited for; matrix products, arithmetic and copies ran while one was open for 16% of the time, Pallas kernels for 0%

commit v1 on v0

v1 whole, which is shorter than its diff:
```python
import math

import jax
import jax.numpy as jnp
from jax import lax
from jax.experimental import pallas as pl
from jax.experimental.pallas import tpu as pltpu
from jax.sharding import PartitionSpec as P

NSFT = 1536
NBIN = 4096
LAGMAX = 16
NLAG = 12
NDET = 3
NGRID = 64
PERIOD = 283
TM = 32
SPAN = 48
FOLD = 288
TURNS = 6
LANES = 128
ROWS = 1792
ZROWS = 304
DEPTH = 2 * NLAG * FOLD
PART = 1024
MESH = pl.DeviceIdType.MESH

COS = (0.9999999890590238, -19.739204499453965, 64.93911745989729, -85.45013953090921,
       60.167630951124465, -25.967599248993793, 6.528658161871135)
SIN = (6.28318527244795, -41.34169703820007, 81.60502363804078, -76.7015376703427,
       42.016075762415646, -14.86832275264805, 3.199338844584104)


def cos_sin(turns):
    u = turns - jnp.floor(turns + 0.5)
    t = u * u
    c = jnp.full_like(t, COS[-1])
    for k in COS[-2::-1]:
        c = c * t + k
    s = jnp.full_like(t, SIN[-1])
    for k in SIN[-2::-1]:
        s = s * t + k
    return c, s * u


def kernel(x_ref, det_ref, tid_ref, inter_ref, lag_ref, o_ref,
           pbuf, idbuf, send_buf, xrecv, osend, orecv,
           xre, xim, det, mat, wl, zc, zs, fac, pairs, pairs_t, acc,
           p_send, p_recv, i_send, i_recv, c_send, c_recv, f_send, o_send, o_recv):
    tm = lax.axis_index("tm")
    h = lax.axis_index("freq")
    core = h % 2
    f32 = jnp.float32
    home = (tm // 8) == h
    own_chunk = jnp.logical_and(home, (tm % 2) == core)
    own_ids = jnp.logical_and(home, (tm % 4) == h)

    barrier = pltpu.get_barrier_semaphore()

    def hail(peer_tm, peer_h, unless):
        @pl.when(jnp.logical_not(unless))
        def _():
            pl.semaphore_signal(barrier, inc=1, device_id=(peer_tm, peer_h), device_id_type=MESH)

    for k in range(8):
        for lo in range(2):
            to_tm, to_h = 8 * h + k, 2 * lo + tm % 2
            hail(to_tm, to_h, jnp.logical_and(to_tm == tm, to_h == h))
    for s in range(16):
        from_tm, from_h = 2 * s + core, tm // 8
        hail(from_tm, from_h, jnp.logical_and(from_tm == tm, from_h == h))
    for d in range(1, 4):
        pl.semaphore_signal(barrier, inc=1, device_id=(tm, (h + d) % 4), device_id_type=MESH)

    re = x_ref[:, 0, :]
    im = x_ref[:, 1, :]
    sq = re * re + im * im
    part = sq[:, 0:LANES]
    for k in range(1, 8):
        part = part + sq[:, k * LANES:(k + 1) * LANES]
    pbuf[h] = part
    idx = tm // 4

    @pl.when(own_chunk)
    def _():
        pl.semaphore_wait(barrier, 33)

    @pl.when(jnp.logical_not(own_chunk))
    def _():
        pl.semaphore_wait(barrier, 35)

    power_copies = []
    for d in range(1, 4):
        copy = pltpu.make_async_remote_copy(
            src_ref=pbuf.at[h], dst_ref=pbuf.at[h], send_sem=p_send.at[d], recv_sem=p_recv.at[4 - d],
            device_id=(tm, (h + d) % 4), device_id_type=MESH)
        copy.start()
        power_copies.append(copy)

    def id_copy(k):
        return pltpu.make_async_remote_copy(
            src_ref=tid_ref, dst_ref=idbuf.at[idx], send_sem=i_send.at[k], recv_sem=i_recv.at[idx],
            device_id=(8 * h + k, tm % 4), device_id_type=MESH)

    def id_is_me(k):
        return jnp.logical_and(8 * h + k == tm, tm % 4 == h)

    for k in range(8):
        @pl.when(jnp.logical_not(id_is_me(k)))
        def _(k=k):
            id_copy(k).start()

    @pl.when(own_ids)
    def _():
        idbuf[idx] = tid_ref[...]

    det[...] = jnp.zeros_like(det)
    for k in range(12):
        row = jnp.broadcast_to(det_ref[k:k + 1, :].astype(f32), (LANES, LANES))
        det[k * LANES:(k + 1) * LANES, :] = row.T

    def mat_rows(b, carry):
        r0 = pl.multiple_of(b * 16, 16)
        d = det[pl.ds(r0, 16), :]
        real = lax.broadcasted_iota(jnp.int32, (16, LANES), 0) + r0 < NSFT
        for e in range(NDET):
            m = jnp.where(d == 0.0, inter_ref[e, 0], jnp.where(d == 1.0, inter_ref[e, 1], inter_ref[e, 2]))
            mat[e, pl.ds(r0, 16), :] = jnp.where(real, m, 0.0)
        return carry

    lax.fori_loop(0, ROWS // 16, mat_rows, 0)

    def weight_rows(b, carry):
        r0 = pl.multiple_of(b * 16, 16)
        d = det[pl.ds(r0, 16), :]
        for l in range(NLAG):
            at = pl.ds(r0 + lag_ref[l], 16)
            wl[l, pl.ds(r0, 16), :] = jnp.where(
                d == 0.0, mat[0, at, :], jnp.where(d == 1.0, mat[1, at, :], mat[2, at, :]))
        return carry

    lax.fori_loop(0, NSFT // 16, weight_rows, 0)
    for l in range(NLAG):
        wl[l, NSFT:, :] = jnp.zeros((ROWS - LAGMAX - NSFT, LANES), f32)
    xre[NSFT:, :] = jnp.zeros((ROWS - NSFT, LANES), f32)
    xim[NSFT:, :] = jnp.zeros((ROWS - NSFT, LANES), f32)

    for copy in power_copies:
        copy.wait()
    power = jnp.sum((pbuf[0] + pbuf[1]) + (pbuf[2] + pbuf[3]), axis=1, keepdims=True) / NBIN
    inv = lax.rsqrt(power + 1e-06)
    re = x_ref[:, 0, :] * inv
    im = x_ref[:, 1, :] * inv
    for k in range(8):
        send_buf[k, 0:SPAN, :] = re[:, k * LANES:(k + 1) * LANES].astype(jnp.bfloat16)
        send_buf[k, SPAN:, :] = im[:, k * LANES:(k + 1) * LANES].astype(jnp.bfloat16)

    def chunk_copy(k, lo):
        return pltpu.make_async_remote_copy(
            src_ref=send_buf.at[k], dst_ref=xrecv.at[tm], send_sem=c_send.at[2 * k + lo], recv_sem=c_recv.at[tm],
            device_id=(8 * h + k, 2 * lo + tm % 2), device_id_type=MESH)

    def chunk_is_me(k, lo):
        return jnp.logical_and(8 * h + k == tm, 2 * lo + tm % 2 == h)

    for k in range(8):
        for lo in range(2):
            @pl.when(jnp.logical_not(chunk_is_me(k, lo)))
            def _(k=k, lo=lo):
                chunk_copy(k, lo).start()

    @pl.when(own_chunk)
    def _():
        xrecv[tm] = send_buf[tm % 8]

    def id_from(s):
        return pltpu.make_async_remote_copy(
            src_ref=tid_ref, dst_ref=idbuf.at[s], send_sem=i_send.at[0], recv_sem=i_recv.at[s],
            device_id=(4 * s + h, tm // 8), device_id_type=MESH)

    for s in range(8):
        @pl.when(jnp.logical_not(jnp.logical_and(4 * s + h == tm, tm // 8 == h)))
        def _(s=s):
            id_from(s).wait_recv()

    for s in range(8):
        ids = idbuf[s].astype(f32)
        amp = (8.0 + 4.0 * ids[0:1, :]) * (0.5 / math.pi)
        cq, sq_ = cos_sin(ids[1:2, :] * (1.0 / NGRID))
        ac = jnp.broadcast_to(amp * cq, (8, LANES))
        as_ = jnp.broadcast_to(amp * sq_, (8, LANES))

        def z_rows(b, carry, s=s, ac=ac, as_=as_):
            r0 = pl.multiple_of(b * 8, 8)
            row = lax.broadcasted_iota(jnp.int32, (8, LANES), 0) + r0
            row = jnp.where(row >= PERIOD, row - PERIOD, row).astype(f32)
            cr, sr = cos_sin(row * (1.0 / PERIOD))
            c, si = cos_sin(sr * ac + cr * as_)
            zc[s, pl.ds(r0, 8), :] = c
            zs[s, pl.ds(r0, 8), :] = si
            return carry

        lax.fori_loop(0, ZROWS // 8, z_rows, 0)

    def factor_rows(n, carry):
        l, b = n // 18, n % 18
        r0 = pl.multiple_of(b * 16, 16)
        lag = lag_ref[l]
        out = pl.multiple_of(l * (2 * FOLD) + r0, 16)
        for s in range(8):
            ci, si = zc[s, pl.ds(r0, 16), :], zs[s, pl.ds(r0, 16), :]
            cj, sj = zc[s, pl.ds(r0 + lag, 16), :], zs[s, pl.ds(r0 + lag, 16), :]
            at = slice(s * LANES, (s + 1) * LANES)
            fac[pl.ds(out, 16), at] = (cj * ci + sj * si).astype(jnp.bfloat16)
            fac[pl.ds(out + FOLD, 16), at] = (sj * ci - cj * si).astype(jnp.bfloat16)
        return carry

    lax.fori_loop(0, NLAG * 18, factor_rows, 0)

    def chunk_from(src):
        return pltpu.make_async_remote_copy(
            src_ref=xrecv.at[src], dst_ref=xrecv.at[src], send_sem=c_send.at[0], recv_sem=c_recv.at[src],
            device_id=(tm, h), device_id_type=MESH)

    def forward(s):
        src = 2 * s + core
        return pltpu.make_async_remote_copy(
            src_ref=xrecv.at[src], dst_ref=xrecv.at[src], send_sem=f_send.at[s], recv_sem=c_recv.at[src],
            device_id=(tm, h + 1 - 2 * core), device_id_type=MESH)

    for s in range(16):
        @pl.when(jnp.logical_not(jnp.logical_and(2 * s + core == tm, tm // 8 == h)))
        def _(s=s):
            pltpu.make_async_remote_copy(
                src_ref=xrecv.at[2 * s + core], dst_ref=xrecv.at[2 * s + core], send_sem=c_send.at[0],
                recv_sem=c_recv.at[2 * s + core], device_id=(2 * s + core, tm // 8),
                device_id_type=MESH).wait_recv()
        forward(s).start()
    for s in range(16):
        pltpu.make_async_remote_copy(
            src_ref=xrecv.at[2 * s + 1 - core], dst_ref=xrecv.at[2 * s + 1 - core], send_sem=f_send.at[s],
            recv_sem=c_recv.at[2 * s + 1 - core], device_id=(tm, h + 1 - 2 * core),
            device_id_type=MESH).wait_recv()

    def unpack(b, carry):
        at = pl.ds(pl.multiple_of(b * SPAN, 16), SPAN)
        xre[at, :] = xrecv[b, 0:SPAN, :].astype(f32)
        xim[at, :] = xrecv[b, SPAN:, :].astype(f32)
        return carry

    lax.fori_loop(0, TM, unpack, 0)

    def pair_rows(n, carry):
        b, l = n // NLAG, n % NLAG
        r0 = pl.multiple_of(b * 16, 16)
        lag = lag_ref[l]
        real = lax.broadcasted_iota(jnp.int32, (16, LANES), 0) + r0 < PERIOD
        sum_re = jnp.zeros((16, LANES), f32)
        sum_im = jnp.zeros((16, LANES), f32)
        for m in range(TURNS):
            here = pl.ds(r0 + PERIOD * m, 16)
            far = pl.ds(r0 + PERIOD * m + lag, 16)
            w = wl[l, here, :]
            a, bb = xre[here, :] * w, xim[here, :] * w
            c, d = xre[far, :], xim[far, :]
            sum_re = sum_re + (a * c + bb * d)
            sum_im = sum_im + (a * d - bb * c)
        out = pl.multiple_of(l * (2 * FOLD) + r0, 16)
        pairs[pl.ds(out, 16), :] = jnp.where(real, sum_re, 0.0)
        pairs[pl.ds(out + FOLD, 16), :] = jnp.where(real, sum_im, 0.0)
        return carry

    lax.fori_loop(0, NLAG * 18, pair_rows, 0)

    def turn(b, carry):
        at = pl.ds(pl.multiple_of(b * LANES, LANES), LANES)
        pairs_t[:, at] = pairs[at, :].T.astype(jnp.bfloat16)
        return carry

    lax.fori_loop(0, DEPTH // LANES, turn, 0)

    acc[...] = jnp.zeros_like(acc)

    def multiply(b, carry):
        at = pl.ds(pl.multiple_of(b * 768, 256), 768)
        acc[...] += jnp.dot(pairs_t[:, at], fac[at, :], preferred_element_type=f32)
        return carry

    lax.fori_loop(0, DEPTH // 768, multiply, 0)

    scale = 1.0 / math.sqrt(NSFT * NLAG)
    group = tm // 8

    def out_copy(s):
        return pltpu.make_async_remote_copy(
            src_ref=osend.at[s], dst_ref=orecv.at[tm % 8], send_sem=o_send.at[s], recv_sem=o_recv.at[tm % 8],
            device_id=(4 * s + h, group), device_id_type=MESH)

    def out_is_me(s):
        return jnp.logical_and(4 * s + h == tm, group == h)

    for s in range(8):
        osend[s] = (acc[:, s * LANES:(s + 1) * LANES].T * scale).astype(jnp.bfloat16)

        @pl.when(jnp.logical_not(out_is_me(s)))
        def _(s=s):
            out_copy(s).start()

    @pl.when(own_ids)
    def _():
        orecv[tm % 8] = osend[tm // 4]

    for k in range(8):
        @pl.when(jnp.logical_not(jnp.logical_and(8 * h + k == tm, tm % 4 == h)))
        def _(k=k):
            pltpu.make_async_remote_copy(
                src_ref=osend.at[k], dst_ref=orecv.at[k], send_sem=o_send.at[k], recv_sem=o_recv.at[k],
                device_id=(8 * h + k, tm % 4), device_id_type=MESH).wait_recv()
        o_ref[:, k * LANES:(k + 1) * LANES] = orecv[k]

    for k in range(8):
        @pl.when(jnp.logical_not(id_is_me(k)))
        def _(k=k):
            id_copy(k).wait_send()
        for lo in range(2):
            @pl.when(jnp.logical_not(chunk_is_me(k, lo)))
            def _(k=k, lo=lo):
                chunk_copy(k, lo).wait_send()

        @pl.when(jnp.logical_not(out_is_me(k)))
        def _(k=k):
            out_copy(k).wait_send()
    for s in range(16):
        forward(s).wait_send()


def shards(sfts, detector_ids, intersection, lags, template_ids):
    bf16, f32 = jnp.bfloat16, jnp.float32
    vmem = pl.BlockSpec(memory_space=pltpu.VMEM)
    smem = pl.BlockSpec(memory_space=pltpu.SMEM)
    dma = pltpu.SemaphoreType.DMA
    out = pl.pallas_call(
        kernel,
        out_shape=jax.ShapeDtypeStruct((LANES, 8 * LANES), bf16),
        in_specs=[vmem, vmem, vmem, smem, smem],
        out_specs=vmem,
        scratch_shapes=[
            pltpu.VMEM((4, SPAN, LANES), f32),
            pltpu.VMEM((8, 2, LANES), jnp.int32),
            pltpu.VMEM((8, 2 * SPAN, LANES), bf16),
            pltpu.VMEM((TM, 2 * SPAN, LANES), bf16),
            pltpu.VMEM((8, LANES, LANES), bf16),
            pltpu.VMEM((8, LANES, LANES), bf16),
            pltpu.VMEM((ROWS, LANES), f32),
            pltpu.VMEM((ROWS, LANES), f32),
            pltpu.VMEM((ROWS + LAGMAX, LANES), f32),
            pltpu.VMEM((NDET, ROWS + LAGMAX, LANES), f32),
            pltpu.VMEM((NLAG, ROWS - LAGMAX, LANES), f32),
            pltpu.VMEM((8, ZROWS, LANES), f32),
            pltpu.VMEM((8, ZROWS, LANES), f32),
            pltpu.VMEM((DEPTH, PART), bf16),
            pltpu.VMEM((DEPTH, LANES), f32),
            pltpu.VMEM((LANES, DEPTH), bf16),
            pltpu.VMEM((LANES, PART), f32),
            dma((4,)), dma((4,)), dma((8,)), dma((8,)), dma((16,)), dma((TM,)), dma((16,)), dma((8,)), dma((8,)),
        ],
        compiler_params=pltpu.CompilerParams(
            collective_id=0, has_side_effects=True, vmem_limit_bytes=60 * 1024 * 1024),
    )(sfts, detector_ids.reshape(12, LANES), template_ids.T, intersection, lags)
    return out.astype(f32)


def solution(mesh):
    in_specs = (P("tm", None, "freq"), P(), P(), P(), P("tm", None))
    out_specs = P("tm", "freq")
    return jax.shard_map(shards, mesh=mesh, in_specs=in_specs, out_specs=out_specs, check_vma=False)
```

time: 369 us -> 65.7 us (0.18)
  the two profiles are of different devices: /device:TPU:0 before, /device:TPU:1 now
where the time goes in v1:
time: 65.7 us; the launch traced here: 65.5 us
  Pallas kernels  63.7 us (97%)
  other arithmetic  1.79 us (3%)
    pallas_call x1, Pallas kernels, shards(): pl.pallas_call(kernel, out_shape=jax.ShapeDtypeStruct((LANES, 8 * LANES),...  63.7 us
    convert_element_type x1, other arithmetic, shards(): return out.astype(f32)  1.79 us

profile of v1, /device:TPU:1, one launch (start us, length us, event | category | flops | bytes accessed | tf_op | source)
XLA Modules:
  0.0 65.5 jit_solution(12087896224169962615)
XLA Ops:
  0.0 63.7 %shard_map.55 = bf16[128,1024]{1,0:T(8,128)(2,1)} custom-call(f32[48,2,1024]{2,1,0:T(2,128)} %x_ref.1, s32[12,128]{1,0:T(8,128)} %bitcast.2, s32[2,128]{1,0:T(2,128)} %bitcast.3, f32[3,3]{1,0:T(4,128)} %inter_ref.1, s32[12]{0:T(128)} %lag_ref.1), custom_call_target="tpu_custom_call" | custom-call | tf_op jit(solution)/shard_map/pallas_call | solution.py:342
  63.7 1.8 %convert_element_type.3 = f32[128,1024]{1,0:T(8,128)} convert(bf16[128,1024]{1,0:T(8,128)(2,1)} %shard_map.55) | non-fusion elementwise | flops 131072 | bytes 786432 | tf_op jit(solution)/shard_map/convert_element_type | solution.py:370

commit v2 on v0

v2 whole, which is shorter than its diff:
```python
import functools
import math

import jax
import jax.numpy as jnp
from jax import lax
from jax.experimental import pallas as pl
from jax.experimental.pallas import tpu as pltpu
from jax.sharding import PartitionSpec as P

NSFT = 1536
NBIN = 4096
LAGMAX = 16
NLAG = 12
NDET = 3
NGRID = 64
PERIOD = 283
TM = 32
SPAN = 48
FOLD = 288
TURNS = 6
LANES = 128
ROWS = 1792
ZROWS = 304
DEPTH = 2 * NLAG * FOLD
PART = 1024
WIDE = 256
MESH = pl.DeviceIdType.MESH

COS = (0.9999999890590238, -19.739204499453965, 64.93911745989729, -85.45013953090921,
       60.167630951124465, -25.967599248993793, 6.528658161871135)
SIN = (6.28318527244795, -41.34169703820007, 81.60502363804078, -76.7015376703427,
       42.016075762415646, -14.86832275264805, 3.199338844584104)


def cos_sin(turns):
    u = turns - jnp.floor(turns + 0.5)
    t = u * u
    c = jnp.full_like(t, COS[-1])
    for k in COS[-2::-1]:
        c = c * t + k
    s = jnp.full_like(t, SIN[-1])
    for k in SIN[-2::-1]:
        s = s * t + k
    return c, s * u


def kernel(x_hbm, det_hbm, tid_hbm, inter_ref, lag_ref, o_ref,
           x_ref, det_ref, tid_ref, pbuf, gsend, gbuf, idbuf, send_buf, xrecv, osend, orecv,
           xre, xim, det, mat, wl, amp_cos, amp_sin, zc, zs, fac, pairs, pairs_t,
           l_sem, p_send, p_recv, i_send, i_recv, g_send, g_recv, c_send, c_recv, fg_send, f_send, o_send, o_recv):
    tm = lax.axis_index("tm")
    h = lax.axis_index("freq")
    core, z_lo = h % 2, h // 2
    x = tm % 4
    f32, bf16 = jnp.float32, jnp.bfloat16

    quarter = (1 - z_lo) * 2 + x % 2
    group = 2 * (x // 2) + core

    def home(k, e):
        return 4 * k + core + 2 * e, (1 - z_lo) * 2 + x % 2

    def source(s):
        return 4 * (s // 2) + 2 * (s % 2) + core, quarter

    def owner(s):
        return 4 * s + group, quarter

    def remote(src, dst, send, recv, to):
        return pltpu.make_async_remote_copy(
            src_ref=src, dst_ref=dst, send_sem=send, recv_sem=recv, device_id=to, device_id_type=MESH)

    barrier = pltpu.get_barrier_semaphore()
    for k in range(8):
        for e in range(2):
            pl.semaphore_signal(barrier, inc=1, device_id=home(k, e), device_id_type=MESH)
    for s in range(16):
        pl.semaphore_signal(barrier, inc=1, device_id=source(s), device_id_type=MESH)
    for d in range(1, 4):
        pl.semaphore_signal(barrier, inc=1, device_id=(tm, (h + d) % 4), device_id_type=MESH)

    det_in = pltpu.make_async_copy(det_hbm, det_ref, l_sem.at[0])
    x_in = pltpu.make_async_copy(x_hbm, x_ref, l_sem.at[1])
    tid_in = pltpu.make_async_copy(tid_hbm, tid_ref, l_sem.at[2])
    det_in.start()
    x_in.start()
    tid_in.start()

    x_in.wait()
    re = x_ref[:, 0, :]
    im = x_ref[:, 1, :]
    sq = re * re + im * im
    part = sq[:, 0:LANES]
    for k in range(1, 8):
        part = part + sq[:, k * LANES:(k + 1) * LANES]
    part = jnp.concatenate([part, jnp.zeros((LANES - SPAN, LANES), f32)], 0)
    pbuf[h] = jnp.sum(part.T, axis=0, keepdims=True)
    for k in range(8):
        send_buf[k, 0:SPAN, :] = re[:, k * LANES:(k + 1) * LANES].astype(bf16)
        send_buf[k, SPAN:, :] = im[:, k * LANES:(k + 1) * LANES].astype(bf16)

    det_in.wait()
    for k in range(12):
        row = jnp.broadcast_to(det_ref[k:k + 1, :].astype(f32), (LANES, LANES))
        det[k * LANES:(k + 1) * LANES, :] = row.T
    for e in range(NDET):
        mat[e, NSFT:, :] = jnp.zeros((ROWS - NSFT, LANES), f32)

    def mat_rows(b, carry):
        at = pl.ds(pl.multiple_of(b * 32, 32), 32)
        d = det[at, :]
        for e in range(NDET):
            mat[e, at, :] = jnp.where(d == 0.0, inter_ref[e, 0], jnp.where(d == 1.0, inter_ref[e, 1], inter_ref[e, 2]))
        return carry

    lax.fori_loop(0, NSFT // 32, mat_rows, 0)

    def weight_rows(b, carry):
        r0 = pl.multiple_of(b * 16, 16)
        d = det[pl.ds(r0, 16), :]
        for l in range(NLAG):
            at = pl.ds(r0 + lag_ref[l], 16)
            wl[l, pl.ds(r0, 16), :] = jnp.where(
                d == 0.0, mat[0, at, :], jnp.where(d == 1.0, mat[1, at, :], mat[2, at, :]))
        return carry

    lax.fori_loop(0, NSFT // 16, weight_rows, 0)
    for l in range(NLAG):
        wl[l, NSFT:, :] = jnp.zeros((ROWS - NSFT, LANES), f32)
    xre[NSFT:, :] = jnp.zeros((ROWS - NSFT, LANES), f32)
    xim[NSFT:, :] = jnp.zeros((ROWS - NSFT, LANES), f32)
    tid_in.wait()

    pl.semaphore_wait(barrier, 35)

    power_copies = [
        remote(pbuf.at[h], pbuf.at[h], p_send.at[d], p_recv.at[4 - d], (tm, (h + d) % 4)) for d in range(1, 4)]
    id_copies = [
        remote(tid_ref, idbuf.at[tm // 4], i_send.at[k], i_recv.at[tm // 4], home(k, x // 2)) for k in range(8)]
    chunk_copies = [
        remote(send_buf.at[k], xrecv.at[tm], c_send.at[2 * k + e], c_recv.at[tm], home(k, e))
        for k in range(8) for e in range(2)]
    for copy in power_copies + id_copies + chunk_copies:
        copy.start()

    for copy in power_copies:
        copy.wait()
    power = ((pbuf[0] + pbuf[1]) + (pbuf[2] + pbuf[3])) / NBIN
    gsend[...] = lax.rsqrt(power + 1e-06)
    scale_copies = [
        remote(gsend, gbuf.at[tm], g_send.at[2 * k + e], g_recv.at[tm], home(k, e))
        for k in range(8) for e in range(2)]
    for copy in scale_copies:
        copy.start()

    for s in range(8):
        remote(tid_ref, idbuf.at[s], i_send.at[s], i_recv.at[s], owner(s)).wait_recv()
    ids = idbuf[...].astype(f32)
    amp = (8.0 + 4.0 * ids[:, 0, :]) * (0.5 / math.pi)
    cq, sq_ = cos_sin(ids[:, 1, :] * (1.0 / NGRID))
    amp_cos[...] = amp * cq
    amp_sin[...] = amp * sq_

    def z_rows(b, carry):
        at = pl.ds(pl.multiple_of(b * 16, 16), 16)
        row = lax.broadcasted_iota(jnp.int32, (16, LANES), 0) + b * 16
        row = jnp.where(row >= PERIOD, row - PERIOD, row).astype(f32)
        cr, sr = cos_sin(row * (1.0 / PERIOD))
        for s in range(8):
            c, si = cos_sin(sr * amp_cos[s:s + 1, :] + cr * amp_sin[s:s + 1, :])
            zc[s, at, :] = c
            zs[s, at, :] = si
        return carry

    lax.fori_loop(0, ZROWS // 16, z_rows, 0)

    def factor_rows(n, carry):
        l, b = n // 9, n % 9
        r0 = pl.multiple_of(b * 32, 32)
        lag = lag_ref[l]
        out = pl.multiple_of(l * (2 * FOLD) + r0, 32)
        for s in range(8):
            ci, si = zc[s, pl.ds(r0, 32), :], zs[s, pl.ds(r0, 32), :]
            cj, sj = zc[s, pl.ds(r0 + lag, 32), :], zs[s, pl.ds(r0 + lag, 32), :]
            at = slice(s * LANES, (s + 1) * LANES)
            fac[pl.ds(out, 32), at] = (cj * ci + sj * si).astype(bf16)
            fac[pl.ds(out + FOLD, 32), at] = (sj * ci - cj * si).astype(bf16)
        return carry

    lax.fori_loop(0, NLAG * 9, factor_rows, 0)

    other = (tm, h + 1 - 2 * core)
    forwards = []
    for s in range(16):
        slot = source(s)[0]
        remote(send_buf.at[0], xrecv.at[slot], c_send.at[s], c_recv.at[slot], source(s)).wait_recv()
        remote(gsend, gbuf.at[slot], g_send.at[s], g_recv.at[slot], source(s)).wait_recv()
        forwards.append(remote(xrecv.at[slot], xrecv.at[slot], f_send.at[s], c_recv.at[slot], other))
        forwards.append(remote(gbuf.at[slot], gbuf.at[slot], fg_send.at[s], g_recv.at[slot], other))
        forwards[-1].start()
        forwards[-2].start()
    for s in range(16):
        slot = source(s)[0] + 1 - 2 * core
        remote(xrecv.at[slot], xrecv.at[slot], f_send.at[s], c_recv.at[slot], other).wait_recv()
        remote(gbuf.at[slot], gbuf.at[slot], fg_send.at[s], g_recv.at[slot], other).wait_recv()

    scales = gbuf[:, 0, :]
    scales = jnp.concatenate([scales, jnp.zeros((LANES - TM, LANES), f32)], 0).T[0:SPAN]
    for b in range(TM):
        g = jnp.broadcast_to(scales[:, b:b + 1], (SPAN, LANES))
        xre[b * SPAN:(b + 1) * SPAN, :] = xrecv[b, 0:SPAN, :].astype(f32) * g
        xim[b * SPAN:(b + 1) * SPAN, :] = xrecv[b, SPAN:, :].astype(f32) * g

    def pair_rows(turns, n, carry):
        b, part = n // 4, n % 4
        r0 = pl.multiple_of(b * 16, 16)
        real = lax.broadcasted_iota(jnp.int32, (16, LANES), 0) + r0 < PERIOD
        lags = [lag_ref[3 * part + q] for q in range(3)]
        sums = [[jnp.zeros((16, LANES), f32)] * 2 for _ in range(3)]
        for m in range(turns):
            here = pl.ds(r0 + PERIOD * m, 16)
            a, bb = xre[here, :], xim[here, :]
            for q in range(3):
                far = pl.ds(r0 + PERIOD * m + lags[q], 16)
                w = wl[3 * part + q, here, :]
                c, d = xre[far, :] * w, xim[far, :] * w
                sums[q] = [sums[q][0] + (a * c + bb * d), sums[q][1] + (a * d - bb * c)]
        for q in range(3):
            out = pl.multiple_of((3 * part + q) * (2 * FOLD) + r0, 16)
            pairs[pl.ds(out, 16), :] = jnp.where(real, sums[q][0], 0.0)
            pairs[pl.ds(out + FOLD, 16), :] = jnp.where(real, sums[q][1], 0.0)
        return carry

    last = (NSFT - PERIOD * (TURNS - 1) + 15) // 16
    lax.fori_loop(0, last * 4, functools.partial(pair_rows, TURNS), 0)
    lax.fori_loop(last * 4, 18 * 4, functools.partial(pair_rows, TURNS - 1), 0)

    def turn(b, carry):
        for q in range(6):
            at = pl.ds(pl.multiple_of((b * 6 + q) * LANES, LANES), LANES)
            pairs_t[:, at] = pairs[at, :].T.astype(bf16)
        return carry

    lax.fori_loop(0, DEPTH // LANES // 6, turn, 0)

    scale = 1.0 / math.sqrt(NSFT * NLAG)

    def multiply(b, carry):
        at = pl.ds(pl.multiple_of(b * WIDE, WIDE), WIDE)
        stat = jnp.dot(pairs_t[...], fac[:, at], preferred_element_type=f32) * scale
        for q in range(2):
            s = 2 * b + q
            osend[s] = stat[:, q * LANES:(q + 1) * LANES].T.astype(bf16)
            remote(osend.at[s], orecv.at[tm // 4], o_send.at[s], o_recv.at[tm // 4], owner(s)).start()
        return carry

    lax.fori_loop(0, PART // WIDE, multiply, 0)

    for k in range(8):
        remote(osend.at[k], orecv.at[k], o_send.at[k], o_recv.at[k], home(k, x // 2)).wait_recv()
        o_ref[:, k * LANES:(k + 1) * LANES] = orecv[k]

    for copy in id_copies + chunk_copies + scale_copies + forwards:
        copy.wait_send()
    for s in range(8):
        remote(osend.at[s], orecv.at[tm // 4], o_send.at[s], o_recv.at[tm // 4], owner(s)).wait_send()


def shards(sfts, detector_ids, intersection, lags, template_ids):
    bf16, f32 = jnp.bfloat16, jnp.float32
    vmem = pl.BlockSpec(memory_space=pltpu.VMEM)
    smem = pl.BlockSpec(memory_space=pltpu.SMEM)
    hbm = pl.BlockSpec(memory_space=pl.ANY)
    dma = pltpu.SemaphoreType.DMA
    out = pl.pallas_call(
        kernel,
        out_shape=jax.ShapeDtypeStruct((LANES, 8 * LANES), bf16),
        in_specs=[hbm, hbm, hbm, smem, smem],
        out_specs=vmem,
        scratch_shapes=[
            pltpu.VMEM((SPAN, 2, 8 * LANES), f32),
            pltpu.VMEM((12, LANES), jnp.int32),
            pltpu.VMEM((2, LANES), jnp.int32),
            pltpu.VMEM((4, 1, LANES), f32),
            pltpu.VMEM((1, LANES), f32),
            pltpu.VMEM((TM, 1, LANES), f32),
            pltpu.VMEM((8, 2, LANES), jnp.int32),
            pltpu.VMEM((8, 2 * SPAN, LANES), bf16),
            pltpu.VMEM((TM, 2 * SPAN, LANES), bf16),
            pltpu.VMEM((8, LANES, LANES), bf16),
            pltpu.VMEM((8, LANES, LANES), bf16),
            pltpu.VMEM((ROWS, LANES), f32),
            pltpu.VMEM((ROWS, LANES), f32),
            pltpu.VMEM((NSFT, LANES), f32),
            pltpu.VMEM((NDET, ROWS, LANES), f32),
            pltpu.VMEM((NLAG, ROWS, LANES), f32),
            pltpu.VMEM((8, LANES), f32),
            pltpu.VMEM((8, LANES), f32),
            pltpu.VMEM((8, ZROWS, LANES), f32),
            pltpu.VMEM((8, ZROWS, LANES), f32),
            pltpu.VMEM((DEPTH, PART), bf16),
            pltpu.VMEM((DEPTH, LANES), f32),
            pltpu.VMEM((LANES, DEPTH), bf16),
            dma((3,)), dma((4,)), dma((4,)), dma((8,)), dma((8,)), dma((16,)), dma((TM,)), dma((16,)), dma((TM,)),
            dma((16,)), dma((16,)), dma((8,)), dma((8,)),
        ],
        compiler_params=pltpu.CompilerParams(
            collective_id=0, has_side_effects=True, vmem_limit_bytes=60 * 1024 * 1024),
    )(sfts, detector_ids.reshape(12, LANES), template_ids.T, intersection, lags)
    return out.astype(f32)


def solution(mesh):
    in_specs = (P("tm", None, "freq"), P(), P(), P(), P("tm", None))
    out_specs = P("tm", "freq")
    return jax.shard_map(shards, mesh=mesh, in_specs=in_specs, out_specs=out_specs, check_vma=False)
```

time: 369 us -> 40.1 us (0.11)
  the two profiles are of different devices: /device:TPU:0 before, /device:TPU:1 now
where the time goes in v2:
time: 40.1 us; the launch traced here: 39.8 us
  Pallas kernels  38 us (95%)
  other arithmetic  1.79 us (4%)
    pallas_call x1, Pallas kernels, shards(): pl.pallas_call(kernel, out_shape=jax.ShapeDtypeStruct((LANES, 8 * LANES),...  38 us
    convert_element_type x1, other arithmetic, shards(): return out.astype(f32)  1.79 us

profile of v2, /device:TPU:1, one launch (start us, length us, event | category | flops | bytes accessed | tf_op | source)
XLA Modules:
  0.0 39.8 jit_solution(17021341218512508968)
XLA Ops:
  0.0 38.0 %shard_map.55 = bf16[128,1024]{1,0:T(8,128)(2,1)} custom-call(f32[48,2,1024]{2,1,0:T(2,128)} %x_hbm.1, s32[12,128]{1,0:T(8,128)} %bitcast.2, s32[2,128]{1,0:T(2,128)} %bitcast.3, f32[3,3]{1,0:T(4,128)} %inter_ref.1, s32[12]{0:T(128)} %lag_ref.1), custom_call_target="tpu_custom_call" | custom-call | tf_op jit(solution)/shard_map/pallas_call | solution.py:276
  38.0 1.8 %convert_element_type.3 = f32[128,1024]{1,0:T(8,128)} convert(bf16[128,1024]{1,0:T(8,128)(2,1)} %shard_map.55) | non-fusion elementwise | flops 131072 | bytes 786432 | tf_op jit(solution)/shard_map/convert_element_type | solution.py:311

commit v3 on v2

--- a/solution.py
+++ b/solution.py
@@ -1,4 +1,3 @@
-import functools
 import math
 
 import jax
@@ -47,7 +46,7 @@
 
 def kernel(x_hbm, det_hbm, tid_hbm, inter_ref, lag_ref, o_ref,
            x_ref, det_ref, tid_ref, pbuf, gsend, gbuf, idbuf, send_buf, xrecv, osend, orecv,
-           xre, xim, det, mat, wl, amp_cos, amp_sin, zc, zs, fac, pairs, pairs_t,
+           xre, xim, det, mat, wl, amp_cos, amp_sin, zc, zs, fac, folded, turned, acc,
            l_sem, p_send, p_recv, i_send, i_recv, g_send, g_recv, c_send, c_recv, fg_send, f_send, o_send, o_recv):
     tm = lax.axis_index("tm")
     h = lax.axis_index("freq")
@@ -176,19 +175,20 @@
     lax.fori_loop(0, ZROWS // 16, z_rows, 0)
 
     def factor_rows(n, carry):
-        l, b = n // 9, n % 9
+        l, b = n // 9 * 2, n % 9
         r0 = pl.multiple_of(b * 32, 32)
-        lag = lag_ref[l]
-        out = pl.multiple_of(l * (2 * FOLD) + r0, 32)
+        lags = lag_ref[l], lag_ref[l + 1]
         for s in range(8):
             ci, si = zc[s, pl.ds(r0, 32), :], zs[s, pl.ds(r0, 32), :]
-            cj, sj = zc[s, pl.ds(r0 + lag, 32), :], zs[s, pl.ds(r0 + lag, 32), :]
-            at = slice(s * LANES, (s + 1) * LANES)
-            fac[pl.ds(out, 32), at] = (cj * ci + sj * si).astype(bf16)
-            fac[pl.ds(out + FOLD, 32), at] = (sj * ci - cj * si).astype(bf16)
-        return carry
-
-    lax.fori_loop(0, NLAG * 9, factor_rows, 0)
+            for q in range(2):
+                far = pl.ds(r0 + lags[q], 32)
+                cj, sj = zc[s, far, :], zs[s, far, :]
+                out = pl.multiple_of((l + q) * (2 * FOLD) + r0, 32)
+                fac[s, pl.ds(out, 32), :] = (cj * ci + sj * si).astype(bf16)
+                fac[s, pl.ds(out + FOLD, 32), :] = (sj * ci - cj * si).astype(bf16)
+        return carry
+
+    lax.fori_loop(0, NLAG // 2 * 9, factor_rows, 0)
 
     other = (tm, h + 1 - 2 * core)
     forwards = []
@@ -212,50 +212,57 @@
         xre[b * SPAN:(b + 1) * SPAN, :] = xrecv[b, 0:SPAN, :].astype(f32) * g
         xim[b * SPAN:(b + 1) * SPAN, :] = xrecv[b, SPAN:, :].astype(f32) * g
 
-    def pair_rows(turns, n, carry):
-        b, part = n // 4, n % 4
-        r0 = pl.multiple_of(b * 16, 16)
-        real = lax.broadcasted_iota(jnp.int32, (16, LANES), 0) + r0 < PERIOD
-        lags = [lag_ref[3 * part + q] for q in range(3)]
-        sums = [[jnp.zeros((16, LANES), f32)] * 2 for _ in range(3)]
-        for m in range(turns):
-            here = pl.ds(r0 + PERIOD * m, 16)
-            a, bb = xre[here, :], xim[here, :]
-            for q in range(3):
-                far = pl.ds(r0 + PERIOD * m + lags[q], 16)
-                w = wl[3 * part + q, here, :]
-                c, d = xre[far, :] * w, xim[far, :] * w
-                sums[q] = [sums[q][0] + (a * c + bb * d), sums[q][1] + (a * d - bb * c)]
-        for q in range(3):
-            out = pl.multiple_of((3 * part + q) * (2 * FOLD) + r0, 16)
-            pairs[pl.ds(out, 16), :] = jnp.where(real, sums[q][0], 0.0)
-            pairs[pl.ds(out + FOLD, 16), :] = jnp.where(real, sums[q][1], 0.0)
-        return carry
-
-    last = (NSFT - PERIOD * (TURNS - 1) + 15) // 16
-    lax.fori_loop(0, last * 4, functools.partial(pair_rows, TURNS), 0)
-    lax.fori_loop(last * 4, 18 * 4, functools.partial(pair_rows, TURNS - 1), 0)
-
-    def turn(b, carry):
-        for q in range(6):
-            at = pl.ds(pl.multiple_of((b * 6 + q) * LANES, LANES), LANES)
-            pairs_t[:, at] = pairs[at, :].T.astype(bf16)
-        return carry
-
-    lax.fori_loop(0, DEPTH // LANES // 6, turn, 0)
+    acc[...] = jnp.zeros_like(acc)
+    turned[...] = jnp.zeros_like(turned)
+
+    def pairs_of(l):
+        lags = lag_ref[l], lag_ref[l + 1]
+        for b in range(FOLD // 16):
+            r0 = 16 * b
+            turns = TURNS if r0 + PERIOD * (TURNS - 1) < NSFT else TURNS - 1
+            sums = [[jnp.zeros((16, LANES), f32)] * 2 for _ in range(2)]
+            for m in range(turns):
+                here = pl.ds(r0 + PERIOD * m, 16)
+                a, bb = xre[here, :], xim[here, :]
+                for q in range(2):
+                    far = pl.ds(r0 + PERIOD * m + lags[q], 16)
+                    w = wl[l + q, here, :]
+                    c, d = xre[far, :], xim[far, :]
+                    sums[q] = [sums[q][0] + (a * c + bb * d) * w, sums[q][1] + (a * d - bb * c) * w]
+            for q in range(2):
+                for p in range(2):
+                    total = sums[q][p]
+                    if r0 + 16 > PERIOD:
+                        real = lax.broadcasted_iota(jnp.int32, (16, LANES), 0) + r0 < PERIOD
+                        total = jnp.where(real, total, 0.0)
+                    at = (2 * q + p) * FOLD + r0
+                    folded[at:at + 16, :] = total
+
+    def turn():
+        for at in range(0, 4 * FOLD, LANES):
+            turned[:, at:at + LANES] = folded[at:at + LANES, :].T.astype(bf16)
+
+    def product(l, n):
+        rows = pl.ds(pl.multiple_of(l * (2 * FOLD), 2 * FOLD), 4 * FOLD)
+        rhs = jnp.concatenate([fac[2 * n, rows, :], fac[2 * n + 1, rows, :]], 1)
+        return acc[:, n * WIDE:(n + 1) * WIDE] + jnp.dot(turned[...], rhs, preferred_element_type=f32)
+
+    def two_lags(i, carry):
+        for n in range(PART // WIDE):
+            acc[:, n * WIDE:(n + 1) * WIDE] = product(jnp.maximum(2 * i - 2, 0), n)
+        pairs_of(2 * i)
+        turn()
+        return carry
+
+    lax.fori_loop(0, NLAG // 2, two_lags, 0)
 
     scale = 1.0 / math.sqrt(NSFT * NLAG)
-
-    def multiply(b, carry):
-        at = pl.ds(pl.multiple_of(b * WIDE, WIDE), WIDE)
-        stat = jnp.dot(pairs_t[...], fac[:, at], preferred_element_type=f32) * scale
+    for n in range(PART // WIDE):
+        stat = product(NLAG - 2, n) * scale
         for q in range(2):
-            s = 2 * b + q
+            s = 2 * n + q
             osend[s] = stat[:, q * LANES:(q + 1) * LANES].T.astype(bf16)
             remote(osend.at[s], orecv.at[tm // 4], o_send.at[s], o_recv.at[tm // 4], owner(s)).start()
-        return carry
-
-    lax.fori_loop(0, PART // WIDE, multiply, 0)
 
     for k in range(8):
         remote(osend.at[k], orecv.at[k], o_send.at[k], o_recv.at[k], home(k, x // 2)).wait_recv()
@@ -299,9 +306,10 @@
             pltpu.VMEM((8, LANES), f32),
             pltpu.VMEM((8, ZROWS, LANES), f32),
             pltpu.VMEM((8, ZROWS, LANES), f32),
-            pltpu.VMEM((DEPTH, PART), bf16),
-            pltpu.VMEM((DEPTH, LANES), f32),
-            pltpu.VMEM((LANES, DEPTH), bf16),
+            pltpu.VMEM((8, DEPTH, LANES), bf16),
+            pltpu.VMEM((4 * FOLD, LANES), f32),
+            pltpu.VMEM((LANES, 4 * FOLD), bf16),
+            pltpu.VMEM((LANES, PART), f32),
             dma((3,)), dma((4,)), dma((4,)), dma((8,)), dma((8,)), dma((16,)), dma((TM,)), dma((16,)), dma((TM,)),
             dma((16,)), dma((16,)), dma((8,)), dma((8,)),
         ],

time: 40.1 us -> 42.7 us (1.065)
  Pallas kernels: 38 us -> 40.6 us
    pallas_call x1, Pallas kernels: 38 us -> 40.6 us  [shards(): pl.pallas_call(kernel, out_shape=jax.ShapeDtypeStruct((LANES, 8 * LANES),...]
where the time goes in v3:
time: 42.7 us; the launch traced here: 42.4 us
  Pallas kernels  40.6 us (95%)
  other arithmetic  1.79 us (4%)
    pallas_call x1, Pallas kernels, shards(): pl.pallas_call(kernel, out_shape=jax.ShapeDtypeStruct((LANES, 8 * LANES),...  40.6 us
    convert_element_type x1, other arithmetic, shards(): return out.astype(f32)  1.79 us

profile of v3, /device:TPU:1, one launch (start us, length us, event | category | flops | bytes accessed | tf_op | source)
XLA Modules:
  0.0 42.4 jit_solution(8867298056213339507)
XLA Ops:
  0.0 40.6 %shard_map.55 = bf16[128,1024]{1,0:T(8,128)(2,1)} custom-call(f32[48,2,1024]{2,1,0:T(2,128)} %x_hbm.1, s32[12,128]{1,0:T(8,128)} %bitcast.2, s32[2,128]{1,0:T(2,128)} %bitcast.3, f32[3,3]{1,0:T(4,128)} %inter_ref.1, s32[12]{0:T(128)} %lag_ref.1), custom_call_target="tpu_custom_call" | custom-call | tf_op jit(solution)/shard_map/pallas_call | solution.py:283
  40.6 1.8 %convert_element_type.3 = f32[128,1024]{1,0:T(8,128)} convert(bf16[128,1024]{1,0:T(8,128)(2,1)} %shard_map.55) | non-fusion elementwise | flops 131072 | bytes 786432 | tf_op jit(solution)/shard_map/convert_element_type | solution.py:319

commit v4 on v2

--- a/solution.py
+++ b/solution.py
@@ -20,7 +20,7 @@
 FOLD = 288
 TURNS = 6
 LANES = 128
-ROWS = 1792
+ROWS = 1600
 ZROWS = 304
 DEPTH = 2 * NLAG * FOLD
 PART = 1024
@@ -45,8 +45,8 @@
     return c, s * u
 
 
-def kernel(x_hbm, det_hbm, tid_hbm, inter_ref, lag_ref, o_ref,
-           x_ref, det_ref, tid_ref, pbuf, gsend, gbuf, idbuf, send_buf, xrecv, osend, orecv,
+def kernel(x_hbm, det_hbm, tid_hbm, inter_hbm, lag_hbm, o_ref,
+           x_ref, det_ref, tid_ref, inter_ref, lag_ref, pbuf, gsend, gbuf, idbuf, send_buf, xrecv, osend, orecv,
            xre, xim, det, mat, wl, amp_cos, amp_sin, zc, zs, fac, pairs, pairs_t,
            l_sem, p_send, p_recv, i_send, i_recv, g_send, g_recv, c_send, c_recv, fg_send, f_send, o_send, o_recv):
     tm = lax.axis_index("tm")
@@ -83,8 +83,12 @@
     det_in = pltpu.make_async_copy(det_hbm, det_ref, l_sem.at[0])
     x_in = pltpu.make_async_copy(x_hbm, x_ref, l_sem.at[1])
     tid_in = pltpu.make_async_copy(tid_hbm, tid_ref, l_sem.at[2])
+    inter_in = pltpu.make_async_copy(inter_hbm, inter_ref, l_sem.at[3])
+    lag_in = pltpu.make_async_copy(lag_hbm, lag_ref, l_sem.at[4])
+    x_in.start()
     det_in.start()
-    x_in.start()
+    inter_in.start()
+    lag_in.start()
     tid_in.start()
 
     x_in.wait()
@@ -101,6 +105,8 @@
         send_buf[k, SPAN:, :] = im[:, k * LANES:(k + 1) * LANES].astype(bf16)
 
     det_in.wait()
+    inter_in.wait()
+    lag_in.wait()
     for k in range(12):
         row = jnp.broadcast_to(det_ref[k:k + 1, :].astype(f32), (LANES, LANES))
         det[k * LANES:(k + 1) * LANES, :] = row.T
@@ -176,19 +182,20 @@
     lax.fori_loop(0, ZROWS // 16, z_rows, 0)
 
     def factor_rows(n, carry):
-        l, b = n // 9, n % 9
+        l, b = n // 9 * 2, n % 9
         r0 = pl.multiple_of(b * 32, 32)
-        lag = lag_ref[l]
-        out = pl.multiple_of(l * (2 * FOLD) + r0, 32)
+        lags = lag_ref[l], lag_ref[l + 1]
         for s in range(8):
             ci, si = zc[s, pl.ds(r0, 32), :], zs[s, pl.ds(r0, 32), :]
-            cj, sj = zc[s, pl.ds(r0 + lag, 32), :], zs[s, pl.ds(r0 + lag, 32), :]
-            at = slice(s * LANES, (s + 1) * LANES)
-            fac[pl.ds(out, 32), at] = (cj * ci + sj * si).astype(bf16)
-            fac[pl.ds(out + FOLD, 32), at] = (sj * ci - cj * si).astype(bf16)
-        return carry
-
-    lax.fori_loop(0, NLAG * 9, factor_rows, 0)
+            for q in range(2):
+                far = pl.ds(r0 + lags[q], 32)
+                cj, sj = zc[s, far, :], zs[s, far, :]
+                out = pl.multiple_of((l + q) * (2 * FOLD) + r0, 32)
+                fac[s, pl.ds(out, 32), :] = (cj * ci + sj * si).astype(bf16)
+                fac[s, pl.ds(out + FOLD, 32), :] = (sj * ci - cj * si).astype(bf16)
+        return carry
+
+    lax.fori_loop(0, NLAG // 2 * 9, factor_rows, 0)
 
     other = (tm, h + 1 - 2 * core)
     forwards = []
@@ -239,7 +246,7 @@
     def turn(b, carry):
         for q in range(6):
             at = pl.ds(pl.multiple_of((b * 6 + q) * LANES, LANES), LANES)
-            pairs_t[:, at] = pairs[at, :].T.astype(bf16)
+            pairs_t[b * 6 + q] = pairs[at, :].T.astype(bf16)
         return carry
 
     lax.fori_loop(0, DEPTH // LANES // 6, turn, 0)
@@ -247,8 +254,9 @@
     scale = 1.0 / math.sqrt(NSFT * NLAG)
 
     def multiply(b, carry):
-        at = pl.ds(pl.multiple_of(b * WIDE, WIDE), WIDE)
-        stat = jnp.dot(pairs_t[...], fac[:, at], preferred_element_type=f32) * scale
+        lhs = jnp.concatenate([pairs_t[k] for k in range(DEPTH // LANES)], 1)
+        rhs = jnp.concatenate([fac[2 * b], fac[2 * b + 1]], 1)
+        stat = jnp.dot(lhs, rhs, preferred_element_type=f32) * scale
         for q in range(2):
             s = 2 * b + q
             osend[s] = stat[:, q * LANES:(q + 1) * LANES].T.astype(bf16)
@@ -257,12 +265,13 @@
 
     lax.fori_loop(0, PART // WIDE, multiply, 0)
 
+    for copy in id_copies + chunk_copies + scale_copies + forwards:
+        copy.wait_send()
+
     for k in range(8):
         remote(osend.at[k], orecv.at[k], o_send.at[k], o_recv.at[k], home(k, x // 2)).wait_recv()
         o_ref[:, k * LANES:(k + 1) * LANES] = orecv[k]
 
-    for copy in id_copies + chunk_copies + scale_copies + forwards:
-        copy.wait_send()
     for s in range(8):
         remote(osend.at[s], orecv.at[tm // 4], o_send.at[s], o_recv.at[tm // 4], owner(s)).wait_send()
 
@@ -270,18 +279,19 @@
 def shards(sfts, detector_ids, intersection, lags, template_ids):
     bf16, f32 = jnp.bfloat16, jnp.float32
     vmem = pl.BlockSpec(memory_space=pltpu.VMEM)
-    smem = pl.BlockSpec(memory_space=pltpu.SMEM)
-    hbm = pl.BlockSpec(memory_space=pl.ANY)
+    hbm = pl.BlockSpec(memory_space=pltpu.HBM)
     dma = pltpu.SemaphoreType.DMA
     out = pl.pallas_call(
         kernel,
         out_shape=jax.ShapeDtypeStruct((LANES, 8 * LANES), bf16),
-        in_specs=[hbm, hbm, hbm, smem, smem],
+        in_specs=[hbm] * 5,
         out_specs=vmem,
         scratch_shapes=[
             pltpu.VMEM((SPAN, 2, 8 * LANES), f32),
             pltpu.VMEM((12, LANES), jnp.int32),
             pltpu.VMEM((2, LANES), jnp.int32),
+            pltpu.SMEM((NDET, NDET), f32),
+            pltpu.SMEM((NLAG,), jnp.int32),
             pltpu.VMEM((4, 1, LANES), f32),
             pltpu.VMEM((1, LANES), f32),
             pltpu.VMEM((TM, 1, LANES), f32),
@@ -299,14 +309,14 @@
             pltpu.VMEM((8, LANES), f32),
             pltpu.VMEM((8, ZROWS, LANES), f32),
             pltpu.VMEM((8, ZROWS, LANES), f32),
-            pltpu.VMEM((DEPTH, PART), bf16),
+            pltpu.VMEM((8, DEPTH, LANES), bf16),
             pltpu.VMEM((DEPTH, LANES), f32),
-            pltpu.VMEM((LANES, DEPTH), bf16),
-            dma((3,)), dma((4,)), dma((4,)), dma((8,)), dma((8,)), dma((16,)), dma((TM,)), dma((16,)), dma((TM,)),
+            pltpu.VMEM((DEPTH // LANES, LANES, LANES), bf16),
+            dma((5,)), dma((4,)), dma((4,)), dma((8,)), dma((8,)), dma((16,)), dma((TM,)), dma((16,)), dma((TM,)),
             dma((16,)), dma((16,)), dma((8,)), dma((8,)),
         ],
         compiler_params=pltpu.CompilerParams(
-            collective_id=0, has_side_effects=True, vmem_limit_bytes=60 * 1024 * 1024),
+            collective_id=0, has_side_effects=True, vmem_limit_bytes=48 * 1024 * 1024),
     )(sfts, detector_ids.reshape(12, LANES), template_ids.T, intersection, lags)
     return out.astype(f32)
 

time: 40.1 us -> 38 us (0.948)
  Pallas kernels: 38 us -> 34.6 us
  local copies, waits for them, and re-layouts: 0 us -> 2.38 us
  other arithmetic: 1.79 us -> 0.84 us
    pallas_call x1, Pallas kernels: 38 us -> 34.6 us  [shards(): pl.pallas_call(kernel, out_shape=jax.ShapeDtypeStruct((LANES, 8 * LANES),...]
    unnamed x0 -> x10, local copies, waits for them, and re-layouts: none -> 2.38 us
    convert_element_type x1, other arithmetic: 1.79 us -> 0.84 us  [shards(): return out.astype(f32)]
where the time goes in v4:
time: 38 us; the launch traced here: 37.8 us
  Pallas kernels  34.6 us (91%)
  local copies, waits for them, and re-layouts  2.38 us (6%)
  other arithmetic  0.84 us (2%)
    pallas_call x1, Pallas kernels, shards(): pl.pallas_call(kernel, out_shape=jax.ShapeDtypeStruct((LANES, 8 * LANES),...  34.6 us
    unnamed x10, local copies, waits for them, and re-layouts  2.38 us
    convert_element_type x1, other arithmetic, shards(): return out.astype(f32)  0.84 us

profile of v4, /device:TPU:1, one launch (start us, length us, event | category | flops | bytes accessed | tf_op | source)
XLA Modules:
  0.0 37.8 jit_solution(13104420009379202690)
XLA Ops:
  0.0 0.0 copy-start.2
  0.0 0.0 copy-start.3
  0.0 0.0 copy-start.4
  0.0 0.7 %copy-done.2 = f32[3,3]{1,0:T(4,128)S(1)} copy-done((f32[3,3]{1,0:T(4,128)S(1)}, f32[3,3]{1,0:T(4,128)}, u32[]{:S(2)}) %copy-start.2) | copy-done | bytes 60
  0.7 0.0 copy-done.3
  0.7 0.0 copy-done.4
  0.7 0.0 copy-start
  0.7 1.0 %copy-done = f32[48,2,1024]{2,1,0:T(2,128)S(1)} copy-done((f32[48,2,1024]{2,1,0:T(2,128)S(1)}, f32[48,2,1024]{2,1,0:T(2,128)}, u32[]{:S(2)}) %copy-start) | copy-done | bytes 393240
  1.7 0.0 copy-start.1
  1.7 0.7 %copy-done.1 = s32[1536]{0:T(1024)S(1)} copy-done((s32[1536]{0:T(1024)S(1)}, s32[1536]{0:T(1024)}, u32[]{:S(2)}) %copy-start.1) | copy-done | bytes 6168
  2.4 34.6 %shard_map.55 = bf16[128,1024]{1,0:T(8,128)(2,1)S(1)} custom-call(f32[48,2,1024]{2,1,0:T(2,128)S(1)} %copy-done, s32[12,128]{1,0:T(8,128)S(1)} %bitcast.2, s32[2,128]{1,0:T(2,128)S(1)} %bitcast.3, f32[3,3]{1,0:T(4,128)S(1)} %copy-done.2, s32[12]{0:T(128)S(1)} %copy-done.4), custom_call_target="tpu_custom_call" | custom-call | tf_op jit(solution)/shard_map/pallas_call | solution.py:284
  37.0 0.8 %convert_element_type.3 = f32[128,1024]{1,0:T(8,128)} convert(bf16[128,1024]{1,0:T(8,128)(2,1)S(1)} %shard_map.55) | non-fusion elementwise | flops 131072 | bytes 786432 | tf_op jit(solution)/shard_map/convert_element_type | solution.py:321
Async XLA Ops:
  0.0 0.7 %copy-start.2 = (f32[3,3]{1,0:T(4,128)S(1)}, f32[3,3]{1,0:T(4,128)}, u32[]{:S(2)}) copy-start(f32[3,3]{1,0:T(4,128)} %inter_hbm.1) | copy-start | bytes 112
  0.0 0.7 %copy-start.3 = (s32[128,2]{0,1:T(2,128)S(1)}, s32[128,2]{0,1:T(2,128)}, u32[]{:S(2)}) copy-start(s32[128,2]{0,1:T(2,128)} %param.9) | copy-start | bytes 3076
  0.0 0.7 %copy-start.4 = (s32[12]{0:T(128)S(1)}, s32[12]{0:T(128)}, u32[]{:S(2)}) copy-start(s32[12]{0:T(128)} %lag_hbm.1) | copy-start | bytes 148
  0.7 1.0 %copy-start = (f32[48,2,1024]{2,1,0:T(2,128)S(1)}, f32[48,2,1024]{2,1,0:T(2,128)}, u32[]{:S(2)}) copy-start(f32[48,2,1024]{2,1,0:T(2,128)} %x_hbm.1) | copy-start | bytes 1179652
  1.7 0.7 %copy-start.1 = (s32[1536]{0:T(1024)S(1)}, s32[1536]{0:T(1024)}, u32[]{:S(2)}) copy-start(s32[1536]{0:T(1024)} %param.6) | copy-start | bytes 18436

commit v5 on v4

v5 whole, which is shorter than its diff:
```python
import functools
import math

import jax
import jax.numpy as jnp
from jax import lax
from jax.experimental import pallas as pl
from jax.experimental.pallas import tpu as pltpu
from jax.sharding import PartitionSpec as P

NSFT = 1536
NBIN = 4096
LAGMAX = 16
NLAG = 12
NDET = 3
NGRID = 64
PERIOD = 283
TM = 32
SPAN = 48
FOLD = 288
TURNS = 6
LANES = 128
HALF = 64
PEERS = 16
ROWS = 1600
ZROWS = 304
DEPTH = NLAG * FOLD
POINTS = 1024
WIDE = 256
MESH = pl.DeviceIdType.MESH

COS = (0.9999999890590238, -19.739204499453965, 64.93911745989729, -85.45013953090921,
       60.167630951124465, -25.967599248993793, 6.528658161871135)
SIN = (6.28318527244795, -41.34169703820007, 81.60502363804078, -76.7015376703427,
       42.016075762415646, -14.86832275264805, 3.199338844584104)


def cos_sin(turns):
    u = turns - jnp.floor(turns + 0.5)
    t = u * u
    c = jnp.full_like(t, COS[-1])
    for k in COS[-2::-1]:
        c = c * t + k
    s = jnp.full_like(t, SIN[-1])
    for k in SIN[-2::-1]:
        s = s * t + k
    return c, s * u


def swapped(v):
    return pltpu.roll(v, HALF, 1)


def low_lanes(rows):
    return lax.broadcasted_iota(jnp.int32, (rows, LANES), 1) < HALF


def kernel(x_hbm, det_hbm, tid_hbm, inter_hbm, lag_hbm, o_ref,
           x_ref, det_ref, tid_ref, inter_ref, lag_ref, pbuf, gsend, gbuf, idbuf, rowbuf, rows_s, upper,
           send_buf, xrecv, table, picked, osend, orecv,
           own, cross, det, mat, wl, zc, zs, fac_c, fac_s, pairs_c, pairs_s, turned_c, turned_s,
           l_sem, p_send, p_recv, i_send, i_recv, g_send, g_recv, c_send, c_recv, fg_send, f_send,
           t_send, t_recv, o_send, o_recv):
    tm = lax.axis_index("tm")
    h = lax.axis_index("freq")
    core, z_lo = h % 2, h // 2
    x = tm % 4
    f32, bf16 = jnp.float32, jnp.bfloat16

    quarter = (1 - z_lo) * 2 + x % 2
    mine = tm // 16 * 8 + tm // 4 % 4 * 2 + x // 2
    slot_of_me = tm // 4 * 2 + x // 2
    other = (tm, h + 1 - 2 * core)

    def home(j):
        return j // 8 * 16 + j // 2 % 4 * 4 + core + j % 2 * 2, (1 - z_lo) * 2 + x % 2

    def source(s):
        return 4 * (s // 2) + 2 * (s % 2) + core, quarter

    def remote(src, dst, send, recv, to):
        return pltpu.make_async_remote_copy(
            src_ref=src, dst_ref=dst, send_sem=send, recv_sem=recv, device_id=to, device_id_type=MESH)

    barrier = pltpu.get_barrier_semaphore()
    for k in range(PEERS):
        pl.semaphore_signal(barrier, inc=1, device_id=home(k), device_id_type=MESH)
        pl.semaphore_signal(barrier, inc=1, device_id=source(k), device_id_type=MESH)
    for d in range(1, 4):
        pl.semaphore_signal(barrier, inc=1, device_id=(tm, (h + d) % 4), device_id_type=MESH)

    x_in = pltpu.make_async_copy(x_hbm, x_ref, l_sem.at[0])
    det_in = pltpu.make_async_copy(det_hbm, det_ref, l_sem.at[1])
    inter_in = pltpu.make_async_copy(inter_hbm, inter_ref, l_sem.at[2])
    lag_in = pltpu.make_async_copy(lag_hbm, lag_ref, l_sem.at[3])
    tid_in = pltpu.make_async_copy(tid_hbm, tid_ref, l_sem.at[4])
    for copy in (x_in, det_in, inter_in, lag_in, tid_in):
        copy.start()

    lane = lax.broadcasted_iota(jnp.int32, (1, LANES), 1)
    cq, sq_ = cos_sin((lane % 32).astype(f32) * (1.0 / NGRID))
    p_low = (lane // 32 + 32 * core).astype(f32)

    def z_rows(b, carry):
        at = pl.ds(pl.multiple_of(b * 16, 16), 16)
        row = lax.broadcasted_iota(jnp.int32, (16, LANES), 0) + b * 16
        row = jnp.where(row >= PERIOD, row - PERIOD, row).astype(f32)
        cr, sr = cos_sin(row * (1.0 / PERIOD))
        sine = (sr * cq + cr * sq_) * (0.5 / math.pi)
        for s in range(8):
            c, si = cos_sin(sine * (8.0 + 4.0 * (p_low + 4.0 * s)))
            zc[s, at, :] = c
            zs[s, at, :] = si
        return carry

    lax.fori_loop(0, ZROWS // 16, z_rows, 0)

    x_in.wait()
    re = x_ref[:, 0, :]
    im = x_ref[:, 1, :]
    sq = re * re + im * im
    part = sq[:, 0:LANES]
    for k in range(1, 8):
        part = part + sq[:, k * LANES:(k + 1) * LANES]
    part = jnp.concatenate([part, jnp.zeros((LANES - SPAN, LANES), f32)], 0)
    pbuf[h] = jnp.sum(part.T, axis=0, keepdims=True)
    low = low_lanes(SPAN)
    for k in range(8):
        r, i = re[:, k * LANES:(k + 1) * LANES], im[:, k * LANES:(k + 1) * LANES]
        send_buf[2 * k] = jnp.where(low, r, swapped(i)).astype(bf16)
        send_buf[2 * k + 1] = jnp.where(low, swapped(r), i).astype(bf16)

    lag_in.wait()

    def factor_rows(n, carry):
        l, b = n // 9 * 2, n % 9
        r0 = pl.multiple_of(b * 32, 32)
        lags = lag_ref[l], lag_ref[l + 1]
        for s in range(8):
            ci, si = zc[s, pl.ds(r0, 32), :], zs[s, pl.ds(r0, 32), :]
            for q in range(2):
                far = pl.ds(r0 + lags[q], 32)
                cj, sj = zc[s, far, :], zs[s, far, :]
                out = pl.ds(pl.multiple_of((l + q) * FOLD + r0, 32), 32)
                fac_c[s, out, :] = (cj * ci + sj * si).astype(bf16)
                fac_s[s, out, :] = (sj * ci - cj * si).astype(bf16)
        return carry

    lax.fori_loop(0, NLAG // 2 * 9, factor_rows, 0)
    tid_in.wait()

    pl.semaphore_wait(barrier, 2 * PEERS + 3)

    power_copies = [
        remote(pbuf.at[h], pbuf.at[h], p_send.at[d], p_recv.at[4 - d], (tm, (h + d) % 4)) for d in range(1, 4)]
    chunk_copies = [
        remote(send_buf.at[k], xrecv.at[tm], c_send.at[k], c_recv.at[tm], home(k)) for k in range(PEERS)]
    id_copies = [
        remote(tid_ref, idbuf.at[slot_of_me], i_send.at[k], i_recv.at[slot_of_me], home(k)) for k in range(PEERS)]
    for copy in power_copies + chunk_copies + id_copies:
        copy.start()

    for copy in power_copies:
        copy.wait()
    power = ((pbuf[0] + pbuf[1]) + (pbuf[2] + pbuf[3])) / NBIN
    gsend[...] = lax.rsqrt(power + 1e-06)
    scale_copies = [
        remote(gsend, gbuf.at[tm], g_send.at[k], g_recv.at[tm], home(k)) for k in range(PEERS)]
    for copy in scale_copies:
        copy.start()

    det_in.wait()
    inter_in.wait()
    for k in range(12):
        row = jnp.broadcast_to(det_ref[k:k + 1, :].astype(f32), (LANES, LANES))
        det[k * LANES:(k + 1) * LANES, :] = row.T
    for e in range(NDET):
        mat[e, NSFT:, :] = jnp.zeros((ROWS - NSFT, LANES), f32)

    def mat_rows(b, carry):
        at = pl.ds(pl.multiple_of(b * 32, 32), 32)
        d = det[at, :]
        for e in range(NDET):
            mat[e, at, :] = jnp.where(d == 0.0, inter_ref[e, 0], jnp.where(d == 1.0, inter_ref[e, 1], inter_ref[e, 2]))
        return carry

    lax.fori_loop(0, NSFT // 32, mat_rows, 0)

    def weight_rows(b, carry):
        r0 = pl.multiple_of(b * 16, 16)
        d = det[pl.ds(r0, 16), :]
        for l in range(NLAG):
            at = pl.ds(r0 + lag_ref[l], 16)
            wl[l, pl.ds(r0, 16), :] = jnp.where(
                d == 0.0, mat[0, at, :], jnp.where(d == 1.0, mat[1, at, :], mat[2, at, :]))
        return carry

    lax.fori_loop(0, NSFT // 16, weight_rows, 0)
    for l in range(NLAG):
        wl[l, NSFT:, :] = jnp.zeros((ROWS - NSFT, LANES), f32)
    own[NSFT:, :] = jnp.zeros((ROWS - NSFT, LANES), f32)
    cross[NSFT:, :] = jnp.zeros((ROWS - NSFT, LANES), f32)

    forwards = []
    for s in range(PEERS):
        slot = source(s)[0]
        remote(send_buf.at[0], xrecv.at[slot], c_send.at[s], c_recv.at[slot], source(s)).wait_recv()
        remote(gsend, gbuf.at[slot], g_send.at[s], g_recv.at[slot], source(s)).wait_recv()
        forwards.append(remote(xrecv.at[slot], xrecv.at[slot], f_send.at[s], c_recv.at[slot], other))
        forwards.append(remote(gbuf.at[slot], gbuf.at[slot], fg_send.at[s], g_recv.at[slot], other))
        forwards[-1].start()
        forwards[-2].start()

    for s in range(PEERS):
        remote(tid_ref, idbuf.at[s], i_send.at[s], i_recv.at[s], source(s)).wait_recv()
    ids = idbuf[...]
    turn_half = ids[:, 1, :] // 32
    rowbuf[...] = ids[:, 0, :] * 32 + (ids[:, 1, :] - 32 * turn_half)
    rows_in = pltpu.make_async_copy(rowbuf, rows_s, l_sem.at[5])
    rows_in.start()
    halves = jnp.concatenate([turn_half.astype(f32), jnp.zeros((LANES - PEERS, LANES), f32)], 0).T
    for s in range(PEERS):
        upper[s] = jnp.broadcast_to(halves[:, s:s + 1], (LANES, LANES))

    for s in range(PEERS):
        slot = source(s)[0] + 1 - 2 * core
        remote(xrecv.at[slot], xrecv.at[slot], f_send.at[s], c_recv.at[slot], other).wait_recv()
        remote(gbuf.at[slot], gbuf.at[slot], fg_send.at[s], g_recv.at[slot], other).wait_recv()

    scales = gbuf[:, 0, :]
    scales = jnp.concatenate([scales, jnp.zeros((LANES - TM, LANES), f32)], 0).T[0:SPAN]
    sign = jnp.where(low, 1.0, -1.0)
    for b in range(TM):
        g = jnp.broadcast_to(scales[:, b:b + 1], (SPAN, LANES))
        v = xrecv[b].astype(f32) * g
        own[b * SPAN:(b + 1) * SPAN, :] = v
        cross[b * SPAN:(b + 1) * SPAN, :] = swapped(v) * sign

    def pair_rows(turns, n, carry):
        b, part = n // 3, n % 3
        r0 = pl.multiple_of(b * 16, 16)
        real = lax.broadcasted_iota(jnp.int32, (16, LANES), 0) + r0 < PERIOD
        lags = [lag_ref[4 * part + q] for q in range(4)]
        sums = [[jnp.zeros((16, LANES), f32)] * 2 for _ in range(4)]
        for m in range(turns):
            here = pl.ds(r0 + PERIOD * m, 16)
            u = own[here, :]
            for q in range(4):
                far = pl.ds(r0 + PERIOD * m + lags[q], 16)
                uw = u * wl[4 * part + q, here, :]
                sums[q] = [sums[q][0] + uw * own[far, :], sums[q][1] + uw * cross[far, :]]
        for q in range(4):
            out = pl.ds(pl.multiple_of((4 * part + q) * FOLD + r0, 16), 16)
            pairs_c[out, :] = jnp.where(real, sums[q][0], 0.0)
            pairs_s[out, :] = jnp.where(real, sums[q][1], 0.0)
        return carry

    last = (NSFT - PERIOD * (TURNS - 1) + 15) // 16
    lax.fori_loop(0, last * 3, functools.partial(pair_rows, TURNS), 0)
    lax.fori_loop(last * 3, 18 * 3, functools.partial(pair_rows, TURNS - 1), 0)

    def turn(b, carry):
        for q in range(3):
            at = pl.ds(pl.multiple_of((b * 3 + q) * LANES, LANES), LANES)
            turned_c[b * 3 + q] = pairs_c[at, :].T.astype(bf16)
            turned_s[b * 3 + q] = pairs_s[at, :].T.astype(bf16)
        return carry

    lax.fori_loop(0, DEPTH // LANES // 3, turn, 0)

    scale = 1.0 / math.sqrt(NSFT * NLAG)

    def swap_copy(b):
        rows = pl.ds(pl.multiple_of(core * POINTS + b * WIDE, WIDE), WIDE)
        return remote(table.at[rows], table.at[rows], t_send.at[b], t_recv.at[b], other)

    def multiply(b, carry):
        sums = []
        for turned, fac in ((turned_c, fac_c), (turned_s, fac_s)):
            lhs = jnp.concatenate([turned[k] for k in range(DEPTH // LANES)], 1)
            rhs = jnp.concatenate([fac[2 * b], fac[2 * b + 1]], 1)
            both = jnp.dot(lhs, rhs, preferred_element_type=f32) * scale
            sums.append(both[0:HALF] + both[HALF:])
        stat = jnp.concatenate([sums[0] + sums[1], sums[0] - sums[1]], 0)
        for q in range(2):
            at = pl.ds(pl.multiple_of(core * POINTS + b * WIDE + q * LANES, LANES), LANES)
            table[at, :] = stat[:, q * LANES:(q + 1) * LANES].T
        swap_copy(b).start()
        return carry

    lax.fori_loop(0, POINTS // WIDE, multiply, 0)

    for copy in id_copies + chunk_copies + scale_copies + forwards:
        copy.wait_send()
    rows_in.wait()
    for b in range(POINTS // WIDE):
        rows = pl.ds(pl.multiple_of((1 - core) * POINTS + b * WIDE, WIDE), WIDE)
        remote(table.at[rows], table.at[rows], t_send.at[b], t_recv.at[b], other).wait_recv()

    low = low_lanes(HALF)

    def serve(s, carry):
        for t in range(LANES):
            picked[t:t + 1, :] = table[pl.ds(rows_s[s, t], 1), :]
        first, second = picked[0:HALF, :], picked[HALF:, :]
        first = jnp.where(upper[s, 0:HALF, :] == 0.0, first, swapped(first))
        second = jnp.where(upper[s, HALF:, :] == 0.0, swapped(second), second)
        osend[s] = jnp.where(low, first, second).astype(bf16)
        remote(osend.at[s], orecv.at[mine], o_send.at[s], o_recv.at[mine], source(s)).start()
        return carry

    lax.fori_loop(0, PEERS, serve, 0)

    for b in range(POINTS // WIDE):
        swap_copy(b).wait_send()
    for k in range(8):
        for j in (2 * k, 2 * k + 1):
            remote(osend.at[j], orecv.at[j], o_send.at[j], o_recv.at[j], home(j)).wait_recv()
        a, b = orecv[2 * k].astype(f32), orecv[2 * k + 1].astype(f32)
        o_ref[0:HALF, k * LANES:(k + 1) * LANES] = jnp.where(low, a, swapped(b)).astype(bf16)
        o_ref[HALF:, k * LANES:(k + 1) * LANES] = jnp.where(low, swapped(a), b).astype(bf16)

    for s in range(PEERS):
        remote(osend.at[s], orecv.at[mine], o_send.at[s], o_recv.at[mine], source(s)).wait_send()


def shards(sfts, detector_ids, intersection, lags, template_ids):
    bf16, f32, i32 = jnp.bfloat16, jnp.float32, jnp.int32
    vmem = pl.BlockSpec(memory_space=pltpu.VMEM)
    hbm = pl.BlockSpec(memory_space=pltpu.HBM)
    dma = pltpu.SemaphoreType.DMA
    out = pl.pallas_call(
        kernel,
        out_shape=jax.ShapeDtypeStruct((LANES, 8 * LANES), bf16),
        in_specs=[hbm] * 5,
        out_specs=vmem,
        scratch_shapes=[
            pltpu.VMEM((SPAN, 2, 8 * LANES), f32),
            pltpu.VMEM((12, LANES), i32),
            pltpu.VMEM((2, LANES), i32),
            pltpu.SMEM((NDET, NDET), f32),
            pltpu.SMEM((NLAG,), i32),
            pltpu.VMEM((4, 1, LANES), f32),
            pltpu.VMEM((1, LANES), f32),
            pltpu.VMEM((TM, 1, LANES), f32),
            pltpu.VMEM((PEERS, 2, LANES), i32),
            pltpu.VMEM((PEERS, LANES), i32),
            pltpu.SMEM((PEERS, LANES), i32),
            pltpu.VMEM((PEERS, LANES, LANES), f32),
            pltpu.VMEM((PEERS, SPAN, LANES), bf16),
            pltpu.VMEM((TM, SPAN, LANES), bf16),
            pltpu.VMEM((2 * POINTS, LANES), f32),
            pltpu.VMEM((LANES, LANES), f32),
            pltpu.VMEM((PEERS, HALF, LANES), bf16),
            pltpu.VMEM((PEERS, HALF, LANES), bf16),
            pltpu.VMEM((ROWS, LANES), f32),
            pltpu.VMEM((ROWS, LANES), f32),
            pltpu.VMEM((NSFT, LANES), f32),
            pltpu.VMEM((NDET, ROWS, LANES), f32),
            pltpu.VMEM((NLAG, ROWS, LANES), f32),
            pltpu.VMEM((8, ZROWS, LANES), f32),
            pltpu.VMEM((8, ZROWS, LANES), f32),
            pltpu.VMEM((8, DEPTH, LANES), bf16),
            pltpu.VMEM((8, DEPTH, LANES), bf16),
            pltpu.VMEM((DEPTH, LANES), f32),
            pltpu.VMEM((DEPTH, LANES), f32),
            pltpu.VMEM((DEPTH // LANES, LANES, LANES), bf16),
            pltpu.VMEM((DEPTH // LANES, LANES, LANES), bf16),
            dma((6,)), dma((4,)), dma((4,)), dma((PEERS,)), dma((PEERS,)), dma((PEERS,)), dma((TM,)),
            dma((PEERS,)), dma((TM,)), dma((PEERS,)), dma((PEERS,)), dma((4,)), dma((4,)), dma((PEERS,)), dma((PEERS,)),
        ],
        compiler_params=pltpu.CompilerParams(
            collective_id=0, has_side_effects=True, vmem_limit_bytes=66_700_000),
    )(sfts, detector_ids.reshape(12, LANES), template_ids.T, intersection, lags)
    return out.astype(f32)


def solution(mesh):
    in_specs = (P("tm", None, "freq"), P(), P(), P(), P("tm", None))
    out_specs = P("tm", "freq")
    return jax.shard_map(shards, mesh=mesh, in_specs=in_specs, out_specs=out_specs, check_vma=False)
```

time: 38 us -> 41.1 us (1.082)
  Pallas kernels: 34.6 us -> 38.8 us
  local copies, waits for them, and re-layouts: 2.38 us -> 0 us
  other arithmetic: 0.84 us -> 1.79 us
    pallas_call x1, Pallas kernels: 34.6 us -> 38.8 us  [shards(): pl.pallas_call(kernel, out_shape=jax.ShapeDtypeStruct((LANES, 8 * LANES),...]
    unnamed x10 -> x0, local copies, waits for them, and re-layouts: 2.38 us -> none
    convert_element_type x1, other arithmetic: 0.84 us -> 1.79 us  [shards(): return out.astype(f32)]
where the time goes in v5:
time: 41.1 us; the launch traced here: 40.6 us
  Pallas kernels  38.8 us (94%)
  other arithmetic  1.79 us (4%)
    pallas_call x1, Pallas kernels, shards(): pl.pallas_call(kernel, out_shape=jax.ShapeDtypeStruct((LANES, 8 * LANES),...  38.8 us
    convert_element_type x1, other arithmetic, shards(): return out.astype(f32)  1.79 us

profile of v5, /device:TPU:1, one launch (start us, length us, event | category | flops | bytes accessed | tf_op | source)
XLA Modules:
  0.0 40.6 jit_solution(3574803761863570496)
XLA Ops:
  0.0 38.8 %shard_map.55 = bf16[128,1024]{1,0:T(8,128)(2,1)} custom-call(f32[48,2,1024]{2,1,0:T(2,128)} %x_hbm.1, s32[12,128]{1,0:T(8,128)} %bitcast.2, s32[2,128]{1,0:T(2,128)} %bitcast.3, f32[3,3]{1,0:T(4,128)} %inter_hbm.1, s32[12]{0:T(128)} %lag_hbm.1), custom_call_target="tpu_custom_call" | custom-call | tf_op jit(solution)/shard_map/pallas_call | solution.py:332
  38.8 1.8 %convert_element_type.3 = f32[128,1024]{1,0:T(8,128)} convert(bf16[128,1024]{1,0:T(8,128)(2,1)} %shard_map.55) | non-fusion elementwise | flops 131072 | bytes 786432 | tf_op jit(solution)/shard_map/convert_element_type | solution.py:375

commit v6 on v4

--- a/solution.py
+++ b/solution.py
@@ -47,7 +47,7 @@
 
 def kernel(x_hbm, det_hbm, tid_hbm, inter_hbm, lag_hbm, o_ref,
            x_ref, det_ref, tid_ref, inter_ref, lag_ref, pbuf, gsend, gbuf, idbuf, send_buf, xrecv, osend, orecv,
-           xre, xim, det, mat, wl, amp_cos, amp_sin, zc, zs, fac, pairs, pairs_t,
+           xre, xim, det, wl, amp_cos, amp_sin, zc, zs, fac, pairs, pairs_t,
            l_sem, p_send, p_recv, i_send, i_recv, g_send, g_recv, c_send, c_recv, fg_send, f_send, o_send, o_recv):
     tm = lax.axis_index("tm")
     h = lax.axis_index("freq")
@@ -92,50 +92,15 @@
     tid_in.start()
 
     x_in.wait()
-    re = x_ref[:, 0, :]
-    im = x_ref[:, 1, :]
-    sq = re * re + im * im
-    part = sq[:, 0:LANES]
-    for k in range(1, 8):
-        part = part + sq[:, k * LANES:(k + 1) * LANES]
+    part = jnp.zeros((SPAN, LANES), f32)
+    for k in range(8):
+        re = x_ref[pl.ds(2 * k, SPAN, stride=16), :]
+        im = x_ref[pl.ds(2 * k + 1, SPAN, stride=16), :]
+        part = part + (re * re + im * im)
+        send_buf[k, 0:SPAN, :] = re.astype(bf16)
+        send_buf[k, SPAN:, :] = im.astype(bf16)
     part = jnp.concatenate([part, jnp.zeros((LANES - SPAN, LANES), f32)], 0)
     pbuf[h] = jnp.sum(part.T, axis=0, keepdims=True)
-    for k in range(8):
-        send_buf[k, 0:SPAN, :] = re[:, k * LANES:(k + 1) * LANES].astype(bf16)
-        send_buf[k, SPAN:, :] = im[:, k * LANES:(k + 1) * LANES].astype(bf16)
-
-    det_in.wait()
-    inter_in.wait()
-    lag_in.wait()
-    for k in range(12):
-        row = jnp.broadcast_to(det_ref[k:k + 1, :].astype(f32), (LANES, LANES))
-        det[k * LANES:(k + 1) * LANES, :] = row.T
-    for e in range(NDET):
-        mat[e, NSFT:, :] = jnp.zeros((ROWS - NSFT, LANES), f32)
-
-    def mat_rows(b, carry):
-        at = pl.ds(pl.multiple_of(b * 32, 32), 32)
-        d = det[at, :]
-        for e in range(NDET):
-            mat[e, at, :] = jnp.where(d == 0.0, inter_ref[e, 0], jnp.where(d == 1.0, inter_ref[e, 1], inter_ref[e, 2]))
-        return carry
-
-    lax.fori_loop(0, NSFT // 32, mat_rows, 0)
-
-    def weight_rows(b, carry):
-        r0 = pl.multiple_of(b * 16, 16)
-        d = det[pl.ds(r0, 16), :]
-        for l in range(NLAG):
-            at = pl.ds(r0 + lag_ref[l], 16)
-            wl[l, pl.ds(r0, 16), :] = jnp.where(
-                d == 0.0, mat[0, at, :], jnp.where(d == 1.0, mat[1, at, :], mat[2, at, :]))
-        return carry
-
-    lax.fori_loop(0, NSFT // 16, weight_rows, 0)
-    for l in range(NLAG):
-        wl[l, NSFT:, :] = jnp.zeros((ROWS - NSFT, LANES), f32)
-    xre[NSFT:, :] = jnp.zeros((ROWS - NSFT, LANES), f32)
-    xim[NSFT:, :] = jnp.zeros((ROWS - NSFT, LANES), f32)
     tid_in.wait()
 
     pl.semaphore_wait(barrier, 35)
@@ -149,6 +114,34 @@
         for k in range(8) for e in range(2)]
     for copy in power_copies + id_copies + chunk_copies:
         copy.start()
+
+    det_in.wait()
+    inter_in.wait()
+    lag_in.wait()
+    det[NSFT:, :] = jnp.full((ROWS - NSFT, LANES), float(NDET), f32)
+    for k in range(12):
+        row = jnp.broadcast_to(det_ref[k:k + 1, :].astype(f32), (LANES, LANES))
+        det[k * LANES:(k + 1) * LANES, :] = row.T
+
+    def weight_rows(last, b, carry):
+        at = pl.ds(pl.multiple_of(b * 16, 16), 16)
+        d = det[at, :]
+        with_far = [
+            jnp.where(d == 0.0, inter_ref[0, e], jnp.where(d == 1.0, inter_ref[1, e], inter_ref[2, e]))
+            for e in range(NDET)]
+        for l in range(NLAG):
+            far = det[pl.ds(b * 16 + lag_ref[l], 16), :]
+            w = jnp.where(far == 0.0, with_far[0], jnp.where(far == 1.0, with_far[1], with_far[2]))
+            wl[l, at, :] = jnp.where(far == float(NDET), 0.0, w) if last else w
+        return carry
+
+    whole = NSFT // 16 - 1
+    lax.fori_loop(0, whole, functools.partial(weight_rows, False), 0)
+    weight_rows(True, whole, 0)
+    for l in range(NLAG):
+        wl[l, NSFT:, :] = jnp.zeros((ROWS - NSFT, LANES), f32)
+    xre[NSFT:, :] = jnp.zeros((ROWS - NSFT, LANES), f32)
+    xim[NSFT:, :] = jnp.zeros((ROWS - NSFT, LANES), f32)
 
     for copy in power_copies:
         copy.wait()
@@ -195,7 +188,7 @@
                 fac[s, pl.ds(out + FOLD, 32), :] = (sj * ci - cj * si).astype(bf16)
         return carry
 
-    lax.fori_loop(0, NLAG // 2 * 9, factor_rows, 0)
+    lax.fori_loop(0, 40, factor_rows, 0)
 
     other = (tm, h + 1 - 2 * core)
     forwards = []
@@ -207,6 +200,8 @@
         forwards.append(remote(gbuf.at[slot], gbuf.at[slot], fg_send.at[s], g_recv.at[slot], other))
         forwards[-1].start()
         forwards[-2].start()
+    lax.fori_loop(40, NLAG // 2 * 9, factor_rows, 0)
+
     for s in range(16):
         slot = source(s)[0] + 1 - 2 * core
         remote(xrecv.at[slot], xrecv.at[slot], f_send.at[s], c_recv.at[slot], other).wait_recv()
@@ -220,28 +215,28 @@
         xim[b * SPAN:(b + 1) * SPAN, :] = xrecv[b, SPAN:, :].astype(f32) * g
 
     def pair_rows(turns, n, carry):
-        b, part = n // 4, n % 4
+        b, part = n // 2, n % 2
         r0 = pl.multiple_of(b * 16, 16)
         real = lax.broadcasted_iota(jnp.int32, (16, LANES), 0) + r0 < PERIOD
-        lags = [lag_ref[3 * part + q] for q in range(3)]
-        sums = [[jnp.zeros((16, LANES), f32)] * 2 for _ in range(3)]
+        lags = [lag_ref[6 * part + q] for q in range(6)]
+        sums = [[jnp.zeros((16, LANES), f32)] * 2 for _ in range(6)]
         for m in range(turns):
             here = pl.ds(r0 + PERIOD * m, 16)
             a, bb = xre[here, :], xim[here, :]
-            for q in range(3):
+            for q in range(6):
                 far = pl.ds(r0 + PERIOD * m + lags[q], 16)
-                w = wl[3 * part + q, here, :]
+                w = wl[6 * part + q, here, :]
                 c, d = xre[far, :] * w, xim[far, :] * w
                 sums[q] = [sums[q][0] + (a * c + bb * d), sums[q][1] + (a * d - bb * c)]
-        for q in range(3):
-            out = pl.multiple_of((3 * part + q) * (2 * FOLD) + r0, 16)
+        for q in range(6):
+            out = pl.multiple_of((6 * part + q) * (2 * FOLD) + r0, 16)
             pairs[pl.ds(out, 16), :] = jnp.where(real, sums[q][0], 0.0)
             pairs[pl.ds(out + FOLD, 16), :] = jnp.where(real, sums[q][1], 0.0)
         return carry
 
     last = (NSFT - PERIOD * (TURNS - 1) + 15) // 16
-    lax.fori_loop(0, last * 4, functools.partial(pair_rows, TURNS), 0)
-    lax.fori_loop(last * 4, 18 * 4, functools.partial(pair_rows, TURNS - 1), 0)
+    lax.fori_loop(0, last * 2, functools.partial(pair_rows, TURNS), 0)
+    lax.fori_loop(last * 2, 18 * 2, functools.partial(pair_rows, TURNS - 1), 0)
 
     def turn(b, carry):
         for q in range(6):
@@ -281,13 +276,14 @@
     vmem = pl.BlockSpec(memory_space=pltpu.VMEM)
     hbm = pl.BlockSpec(memory_space=pltpu.HBM)
     dma = pltpu.SemaphoreType.DMA
+    rows = sfts.reshape(SPAN, 2, 8, LANES).transpose(0, 2, 1, 3).reshape(SPAN * 16, LANES)
     out = pl.pallas_call(
         kernel,
-        out_shape=jax.ShapeDtypeStruct((LANES, 8 * LANES), bf16),
+        out_shape=pltpu.VMEM((LANES, 8 * LANES), bf16),
         in_specs=[hbm] * 5,
         out_specs=vmem,
         scratch_shapes=[
-            pltpu.VMEM((SPAN, 2, 8 * LANES), f32),
+            pltpu.VMEM((SPAN * 16, LANES), f32),
             pltpu.VMEM((12, LANES), jnp.int32),
             pltpu.VMEM((2, LANES), jnp.int32),
             pltpu.SMEM((NDET, NDET), f32),
@@ -302,8 +298,7 @@
             pltpu.VMEM((8, LANES, LANES), bf16),
             pltpu.VMEM((ROWS, LANES), f32),
             pltpu.VMEM((ROWS, LANES), f32),
-            pltpu.VMEM((NSFT, LANES), f32),
-            pltpu.VMEM((NDET, ROWS, LANES), f32),
+            pltpu.VMEM((ROWS, LANES), f32),
             pltpu.VMEM((NLAG, ROWS, LANES), f32),
             pltpu.VMEM((8, LANES), f32),
             pltpu.VMEM((8, LANES), f32),
@@ -316,8 +311,8 @@
             dma((16,)), dma((16,)), dma((8,)), dma((8,)),
         ],
         compiler_params=pltpu.CompilerParams(
-            collective_id=0, has_side_effects=True, vmem_limit_bytes=48 * 1024 * 1024),
-    )(sfts, detector_ids.reshape(12, LANES), template_ids.T, intersection, lags)
+            collective_id=0, has_side_effects=True, vmem_limit_bytes=60 * 1024 * 1024),
+    )(rows, detector_ids.reshape(12, LANES), template_ids.T, intersection, lags)
     return out.astype(f32)
 
 

time: 38 us -> 35.6 us (0.937)
  local copies, waits for them, and re-layouts: 2.38 us -> 0 us
    unnamed x10 -> x0, local copies, waits for them, and re-layouts: 2.38 us -> none
where the time goes in v6:
time: 35.6 us; the launch traced here: 35.4 us
  Pallas kernels  34.6 us (97%)
  other arithmetic  0.84 us (2%)
    pallas_call x1, Pallas kernels, shards(): pl.pallas_call(kernel, out_shape=pltpu.VMEM((LANES, 8 * LANES), bf16), in...  34.6 us
    convert_element_type x1, other arithmetic, shards(): return out.astype(f32)  0.84 us

profile of v6, /device:TPU:1, one launch (start us, length us, event | category | flops | bytes accessed | tf_op | source)
XLA Modules:
  0.0 35.4 jit_solution(14812516669524237950)
XLA Ops:
  0.0 34.6 %shard_map.55 = bf16[128,1024]{1,0:T(8,128)(2,1)S(1)} custom-call(f32[768,128]{1,0:T(8,128)} %bitcast.7, s32[12,128]{1,0:T(8,128)} %bitcast.8, s32[2,128]{1,0:T(2,128)} %bitcast.9, f32[3,3]{1,0:T(4,128)} %inter_hbm.1, s32[12]{0:T(128)} %lag_hbm.1), custom_call_target="tpu_custom_call" | custom-call | tf_op jit(solution)/shard_map/pallas_call | solution.py:280
  34.6 0.8 %convert_element_type.3 = f32[128,1024]{1,0:T(8,128)} convert(bf16[128,1024]{1,0:T(8,128)(2,1)S(1)} %shard_map.55) | non-fusion elementwise | flops 131072 | bytes 786432 | tf_op jit(solution)/shard_map/convert_element_type | solution.py:316

commit v7 on v6

--- a/solution.py
+++ b/solution.py
@@ -21,7 +21,7 @@
 TURNS = 6
 LANES = 128
 ROWS = 1600
-ZROWS = 304
+ZROWS = 320
 DEPTH = 2 * NLAG * FOLD
 PART = 1024
 WIDE = 256
@@ -47,7 +47,7 @@
 
 def kernel(x_hbm, det_hbm, tid_hbm, inter_hbm, lag_hbm, o_ref,
            x_ref, det_ref, tid_ref, inter_ref, lag_ref, pbuf, gsend, gbuf, idbuf, send_buf, xrecv, osend, orecv,
-           xre, xim, det, wl, amp_cos, amp_sin, zc, zs, fac, pairs, pairs_t,
+           xre, xim, det, wl, amp_cos, amp_sin, orbit_cos, orbit_sin, zc, zs, fac, pairs, pairs_t,
            l_sem, p_send, p_recv, i_send, i_recv, g_send, g_recv, c_send, c_recv, fg_send, f_send, o_send, o_recv):
     tm = lax.axis_index("tm")
     h = lax.axis_index("freq")
@@ -64,8 +64,13 @@
     def source(s):
         return 4 * (s // 2) + 2 * (s % 2) + core, quarter
 
-    def owner(s):
-        return 4 * s + group, quarter
+    y = tm // 4 % 4
+
+    def owner(p):
+        return p % 2 * 16 + (y + p // 2 + 2) % 4 * 4 + group, quarter
+
+    def place(to):
+        return (y - to[0] // 4 % 4 + 2) % 4 * 2 + tm // 16
 
     def remote(src, dst, send, recv, to):
         return pltpu.make_async_remote_copy(
@@ -108,11 +113,12 @@
     power_copies = [
         remote(pbuf.at[h], pbuf.at[h], p_send.at[d], p_recv.at[4 - d], (tm, (h + d) % 4)) for d in range(1, 4)]
     id_copies = [
-        remote(tid_ref, idbuf.at[tm // 4], i_send.at[k], i_recv.at[tm // 4], home(k, x // 2)) for k in range(8)]
+        remote(tid_ref, idbuf.at[place(home(k, x // 2))], i_send.at[k], i_recv.at[place(home(k, x // 2))], home(k, x // 2))
+        for k in range(8)]
     chunk_copies = [
         remote(send_buf.at[k], xrecv.at[tm], c_send.at[2 * k + e], c_recv.at[tm], home(k, e))
-        for k in range(8) for e in range(2)]
-    for copy in power_copies + id_copies + chunk_copies:
+        for e in range(2) for k in range(8)]
+    for copy in power_copies + id_copies + chunk_copies[:8]:
         copy.start()
 
     det_in.wait()
@@ -150,45 +156,49 @@
     scale_copies = [
         remote(gsend, gbuf.at[tm], g_send.at[2 * k + e], g_recv.at[tm], home(k, e))
         for k in range(8) for e in range(2)]
-    for copy in scale_copies:
+    for copy in scale_copies + chunk_copies[8:]:
         copy.start()
 
-    for s in range(8):
+    def orbit_rows(b, carry):
+        at = pl.ds(pl.multiple_of(b * 64, 64), 64)
+        row = lax.broadcasted_iota(jnp.int32, (64, LANES), 0) + b * 64
+        row = jnp.where(row >= PERIOD, row - PERIOD, row).astype(f32)
+        orbit_cos[at, :], orbit_sin[at, :] = cos_sin(row * (1.0 / PERIOD))
+        return carry
+
+    lax.fori_loop(0, ZROWS // 64, orbit_rows, 0)
+
+    def factors(s):
         remote(tid_ref, idbuf.at[s], i_send.at[s], i_recv.at[s], owner(s)).wait_recv()
-    ids = idbuf[...].astype(f32)
-    amp = (8.0 + 4.0 * ids[:, 0, :]) * (0.5 / math.pi)
-    cq, sq_ = cos_sin(ids[:, 1, :] * (1.0 / NGRID))
-    amp_cos[...] = amp * cq
-    amp_sin[...] = amp * sq_
-
-    def z_rows(b, carry):
-        at = pl.ds(pl.multiple_of(b * 16, 16), 16)
-        row = lax.broadcasted_iota(jnp.int32, (16, LANES), 0) + b * 16
-        row = jnp.where(row >= PERIOD, row - PERIOD, row).astype(f32)
-        cr, sr = cos_sin(row * (1.0 / PERIOD))
-        for s in range(8):
-            c, si = cos_sin(sr * amp_cos[s:s + 1, :] + cr * amp_sin[s:s + 1, :])
-            zc[s, at, :] = c
-            zs[s, at, :] = si
-        return carry
-
-    lax.fori_loop(0, ZROWS // 16, z_rows, 0)
-
-    def factor_rows(n, carry):
-        l, b = n // 9 * 2, n % 9
-        r0 = pl.multiple_of(b * 32, 32)
-        lags = lag_ref[l], lag_ref[l + 1]
-        for s in range(8):
+        ids = idbuf[s].astype(f32)
+        amp = (8.0 + 4.0 * ids[0:1, :]) * (0.5 / math.pi)
+        cq, sq_ = cos_sin(ids[1:2, :] * (1.0 / NGRID))
+        amp_cos[...] = jnp.broadcast_to(amp * cq, (8, LANES))
+        amp_sin[...] = jnp.broadcast_to(amp * sq_, (8, LANES))
+
+        def z_rows(b, carry):
+            at = pl.ds(pl.multiple_of(b * 64, 64), 64)
+            turns = orbit_sin[at, :] * amp_cos[0:1, :] + orbit_cos[at, :] * amp_sin[0:1, :]
+            zc[s, at, :], zs[s, at, :] = cos_sin(turns)
+            return carry
+
+        lax.fori_loop(0, ZROWS // 64, z_rows, 0)
+
+        def factor_rows(b, carry):
+            r0 = pl.multiple_of(b * 32, 32)
             ci, si = zc[s, pl.ds(r0, 32), :], zs[s, pl.ds(r0, 32), :]
-            for q in range(2):
-                far = pl.ds(r0 + lags[q], 32)
+            for l in range(NLAG):
+                far = pl.ds(r0 + lag_ref[l], 32)
                 cj, sj = zc[s, far, :], zs[s, far, :]
-                out = pl.multiple_of((l + q) * (2 * FOLD) + r0, 32)
+                out = pl.multiple_of(l * (2 * FOLD) + r0, 32)
                 fac[s, pl.ds(out, 32), :] = (cj * ci + sj * si).astype(bf16)
                 fac[s, pl.ds(out + FOLD, 32), :] = (sj * ci - cj * si).astype(bf16)
-        return carry
-
-    lax.fori_loop(0, 40, factor_rows, 0)
+            return carry
+
+        lax.fori_loop(0, FOLD // 32, factor_rows, 0)
+
+    for s in (4, 5, 6, 7, 2, 3, 0):
+        factors(s)
 
     other = (tm, h + 1 - 2 * core)
     forwards = []
@@ -200,7 +210,7 @@
         forwards.append(remote(gbuf.at[slot], gbuf.at[slot], fg_send.at[s], g_recv.at[slot], other))
         forwards[-1].start()
         forwards[-2].start()
-    lax.fori_loop(40, NLAG // 2 * 9, factor_rows, 0)
+    factors(1)
 
     for s in range(16):
         slot = source(s)[0] + 1 - 2 * core
@@ -248,7 +258,8 @@
 
     scale = 1.0 / math.sqrt(NSFT * NLAG)
 
-    def multiply(b, carry):
+    def multiply(n, carry):
+        b = n + n // 2 * (1 - n % 2 * 2)
         lhs = jnp.concatenate([pairs_t[k] for k in range(DEPTH // LANES)], 1)
         rhs = jnp.concatenate([fac[2 * b], fac[2 * b + 1]], 1)
         stat = jnp.dot(lhs, rhs, preferred_element_type=f32) * scale
@@ -302,6 +313,8 @@
             pltpu.VMEM((NLAG, ROWS, LANES), f32),
             pltpu.VMEM((8, LANES), f32),
             pltpu.VMEM((8, LANES), f32),
+            pltpu.VMEM((ZROWS, LANES), f32),
+            pltpu.VMEM((ZROWS, LANES), f32),
             pltpu.VMEM((8, ZROWS, LANES), f32),
             pltpu.VMEM((8, ZROWS, LANES), f32),
             pltpu.VMEM((8, DEPTH, LANES), bf16),

time: 35.6 us -> 35.9 us (level)
  the two profiles are of different devices: /device:TPU:1 before, /device:TPU:5 now
where the time goes in v7:
time: 35.9 us; the launch traced here: 35.7 us
  Pallas kernels  34.9 us (97%)
  other arithmetic  0.84 us (2%)
    pallas_call x1, Pallas kernels, shards(): pl.pallas_call(kernel, out_shape=pltpu.VMEM((LANES, 8 * LANES), bf16), in...  34.9 us
    convert_element_type x1, other arithmetic, shards(): return out.astype(f32)  0.84 us

profile of v7, /device:TPU:5, one launch (start us, length us, event | category | flops | bytes accessed | tf_op | source)
XLA Modules:
  0.0 35.7 jit_solution(16813418205710157191)
XLA Ops:
  0.0 34.9 %shard_map.55 = bf16[128,1024]{1,0:T(8,128)(2,1)S(1)} custom-call(f32[768,128]{1,0:T(8,128)} %bitcast.7, s32[12,128]{1,0:T(8,128)} %bitcast.8, s32[2,128]{1,0:T(2,128)} %bitcast.9, f32[3,3]{1,0:T(4,128)} %inter_hbm.1, s32[12]{0:T(128)} %lag_hbm.1), custom_call_target="tpu_custom_call" | custom-call | tf_op jit(solution)/shard_map/pallas_call | solution.py:291
  34.9 0.8 %convert_element_type.3 = f32[128,1024]{1,0:T(8,128)} convert(bf16[128,1024]{1,0:T(8,128)(2,1)S(1)} %shard_map.55) | non-fusion elementwise | flops 131072 | bytes 786432 | tf_op jit(solution)/shard_map/convert_element_type | solution.py:329

commit v8 on v7

--- a/solution.py
+++ b/solution.py
@@ -67,10 +67,10 @@
     y = tm // 4 % 4
 
     def owner(p):
-        return p % 2 * 16 + (y + p // 2 + 2) % 4 * 4 + group, quarter
+        return 4 * p + group, quarter
 
     def place(to):
-        return (y - to[0] // 4 % 4 + 2) % 4 * 2 + tm // 16
+        return tm // 4
 
     def remote(src, dst, send, recv, to):
         return pltpu.make_async_remote_copy(
@@ -118,7 +118,7 @@
     chunk_copies = [
         remote(send_buf.at[k], xrecv.at[tm], c_send.at[2 * k + e], c_recv.at[tm], home(k, e))
         for e in range(2) for k in range(8)]
-    for copy in power_copies + id_copies + chunk_copies[:8]:
+    for copy in power_copies + id_copies + chunk_copies[:12]:
         copy.start()
 
     det_in.wait()
@@ -142,7 +142,7 @@
         return carry
 
     whole = NSFT // 16 - 1
-    lax.fori_loop(0, whole, functools.partial(weight_rows, False), 0)
+    lax.fori_loop(0, 40, functools.partial(weight_rows, False), 0)
     weight_rows(True, whole, 0)
     for l in range(NLAG):
         wl[l, NSFT:, :] = jnp.zeros((ROWS - NSFT, LANES), f32)
@@ -156,8 +156,9 @@
     scale_copies = [
         remote(gsend, gbuf.at[tm], g_send.at[2 * k + e], g_recv.at[tm], home(k, e))
         for k in range(8) for e in range(2)]
-    for copy in scale_copies + chunk_copies[8:]:
+    for copy in scale_copies + chunk_copies[12:]:
         copy.start()
+    lax.fori_loop(40, whole, functools.partial(weight_rows, False), 0)
 
     def orbit_rows(b, carry):
         at = pl.ds(pl.multiple_of(b * 64, 64), 64)
@@ -259,7 +260,7 @@
     scale = 1.0 / math.sqrt(NSFT * NLAG)
 
     def multiply(n, carry):
-        b = n + n // 2 * (1 - n % 2 * 2)
+        b = n
         lhs = jnp.concatenate([pairs_t[k] for k in range(DEPTH // LANES)], 1)
         rhs = jnp.concatenate([fac[2 * b], fac[2 * b + 1]], 1)
         stat = jnp.dot(lhs, rhs, preferred_element_type=f32) * scale

time: 35.9 us -> 33.8 us (0.942)
  the two profiles are of different devices: /device:TPU:5 before, /device:TPU:1 now
where the time goes in v8:
time: 33.8 us; the launch traced here: 33.7 us
  Pallas kernels  32.8 us (97%)
  other arithmetic  0.84 us (2%)
    pallas_call x1, Pallas kernels, shards(): pl.pallas_call(kernel, out_shape=pltpu.VMEM((LANES, 8 * LANES), bf16), in...  32.8 us
    convert_element_type x1, other arithmetic, shards(): return out.astype(f32)  0.84 us

profile of v8, /device:TPU:1, one launch (start us, length us, event | category | flops | bytes accessed | tf_op | source)
XLA Modules:
  0.0 33.7 jit_solution(12302157295337941812)
XLA Ops:
  0.0 32.8 %shard_map.55 = bf16[128,1024]{1,0:T(8,128)(2,1)S(1)} custom-call(f32[768,128]{1,0:T(8,128)} %bitcast.7, s32[12,128]{1,0:T(8,128)} %bitcast.8, s32[2,128]{1,0:T(2,128)} %bitcast.9, f32[3,3]{1,0:T(4,128)} %inter_hbm.1, s32[12]{0:T(128)} %lag_hbm.1), custom_call_target="tpu_custom_call" | custom-call | tf_op jit(solution)/shard_map/pallas_call | solution.py:292
  32.9 0.8 %convert_element_type.3 = f32[128,1024]{1,0:T(8,128)} convert(bf16[128,1024]{1,0:T(8,128)(2,1)S(1)} %shard_map.55) | non-fusion elementwise | flops 131072 | bytes 786432 | tf_op jit(solution)/shard_map/convert_element_type | solution.py:330

commit v9 on v8

--- a/solution.py
+++ b/solution.py
@@ -76,15 +76,6 @@
         return pltpu.make_async_remote_copy(
             src_ref=src, dst_ref=dst, send_sem=send, recv_sem=recv, device_id=to, device_id_type=MESH)
 
-    barrier = pltpu.get_barrier_semaphore()
-    for k in range(8):
-        for e in range(2):
-            pl.semaphore_signal(barrier, inc=1, device_id=home(k, e), device_id_type=MESH)
-    for s in range(16):
-        pl.semaphore_signal(barrier, inc=1, device_id=source(s), device_id_type=MESH)
-    for d in range(1, 4):
-        pl.semaphore_signal(barrier, inc=1, device_id=(tm, (h + d) % 4), device_id_type=MESH)
-
     det_in = pltpu.make_async_copy(det_hbm, det_ref, l_sem.at[0])
     x_in = pltpu.make_async_copy(x_hbm, x_ref, l_sem.at[1])
     tid_in = pltpu.make_async_copy(tid_hbm, tid_ref, l_sem.at[2])
@@ -96,6 +87,15 @@
     lag_in.start()
     tid_in.start()
 
+    barrier = pltpu.get_barrier_semaphore()
+    for k in range(8):
+        for e in range(2):
+            pl.semaphore_signal(barrier, inc=1, device_id=home(k, e), device_id_type=MESH)
+    for s in range(16):
+        pl.semaphore_signal(barrier, inc=1, device_id=source(s), device_id_type=MESH)
+    for d in range(1, 4):
+        pl.semaphore_signal(barrier, inc=1, device_id=(tm, (h + d) % 4), device_id_type=MESH)
+
     x_in.wait()
     part = jnp.zeros((SPAN, LANES), f32)
     for k in range(8):
@@ -106,6 +106,43 @@
         send_buf[k, SPAN:, :] = im.astype(bf16)
     part = jnp.concatenate([part, jnp.zeros((LANES - SPAN, LANES), f32)], 0)
     pbuf[h] = jnp.sum(part.T, axis=0, keepdims=True)
+    det_in.wait()
+    inter_in.wait()
+    lag_in.wait()
+    det[NSFT:, :] = jnp.full((ROWS - NSFT, LANES), float(NDET), f32)
+    for k in range(12):
+        row = jnp.broadcast_to(det_ref[k:k + 1, :].astype(f32), (LANES, LANES))
+        det[k * LANES:(k + 1) * LANES, :] = row.T
+
+    def weight_rows(last, b, carry):
+        at = pl.ds(pl.multiple_of(b * 16, 16), 16)
+        d = det[at, :]
+        with_far = [
+            jnp.where(d == 0.0, inter_ref[0, e], jnp.where(d == 1.0, inter_ref[1, e], inter_ref[2, e]))
+            for e in range(NDET)]
+        for l in range(NLAG):
+            far = det[pl.ds(b * 16 + lag_ref[l], 16), :]
+            w = jnp.where(far == 0.0, with_far[0], jnp.where(far == 1.0, with_far[1], with_far[2]))
+            wl[l, at, :] = jnp.where(far == float(NDET), 0.0, w) if last else w
+        return carry
+
+    whole = NSFT // 16 - 1
+    lax.fori_loop(0, 40, functools.partial(weight_rows, False), 0)
+    weight_rows(True, whole, 0)
+    for l in range(NLAG):
+        wl[l, NSFT:, :] = jnp.zeros((ROWS - NSFT, LANES), f32)
+    xre[NSFT:, :] = jnp.zeros((ROWS - NSFT, LANES), f32)
+    xim[NSFT:, :] = jnp.zeros((ROWS - NSFT, LANES), f32)
+
+    def orbit_rows(b, carry):
+        at = pl.ds(pl.multiple_of(b * 64, 64), 64)
+        row = lax.broadcasted_iota(jnp.int32, (64, LANES), 0) + b * 64
+        row = jnp.where(row >= PERIOD, row - PERIOD, row).astype(f32)
+        orbit_cos[at, :], orbit_sin[at, :] = cos_sin(row * (1.0 / PERIOD))
+        return carry
+
+    lax.fori_loop(0, ZROWS // 64, orbit_rows, 0)
+
     tid_in.wait()
 
     pl.semaphore_wait(barrier, 35)
@@ -121,34 +158,6 @@
     for copy in power_copies + id_copies + chunk_copies[:12]:
         copy.start()
 
-    det_in.wait()
-    inter_in.wait()
-    lag_in.wait()
-    det[NSFT:, :] = jnp.full((ROWS - NSFT, LANES), float(NDET), f32)
-    for k in range(12):
-        row = jnp.broadcast_to(det_ref[k:k + 1, :].astype(f32), (LANES, LANES))
-        det[k * LANES:(k + 1) * LANES, :] = row.T
-
-    def weight_rows(last, b, carry):
-        at = pl.ds(pl.multiple_of(b * 16, 16), 16)
-        d = det[at, :]
-        with_far = [
-            jnp.where(d == 0.0, inter_ref[0, e], jnp.where(d == 1.0, inter_ref[1, e], inter_ref[2, e]))
-            for e in range(NDET)]
-        for l in range(NLAG):
-            far = det[pl.ds(b * 16 + lag_ref[l], 16), :]
-            w = jnp.where(far == 0.0, with_far[0], jnp.where(far == 1.0, with_far[1], with_far[2]))
-            wl[l, at, :] = jnp.where(far == float(NDET), 0.0, w) if last else w
-        return carry
-
-    whole = NSFT // 16 - 1
-    lax.fori_loop(0, 40, functools.partial(weight_rows, False), 0)
-    weight_rows(True, whole, 0)
-    for l in range(NLAG):
-        wl[l, NSFT:, :] = jnp.zeros((ROWS - NSFT, LANES), f32)
-    xre[NSFT:, :] = jnp.zeros((ROWS - NSFT, LANES), f32)
-    xim[NSFT:, :] = jnp.zeros((ROWS - NSFT, LANES), f32)
-
     for copy in power_copies:
         copy.wait()
     power = ((pbuf[0] + pbuf[1]) + (pbuf[2] + pbuf[3])) / NBIN
@@ -159,15 +168,6 @@
     for copy in scale_copies + chunk_copies[12:]:
         copy.start()
     lax.fori_loop(40, whole, functools.partial(weight_rows, False), 0)
-
-    def orbit_rows(b, carry):
-        at = pl.ds(pl.multiple_of(b * 64, 64), 64)
-        row = lax.broadcasted_iota(jnp.int32, (64, LANES), 0) + b * 64
-        row = jnp.where(row >= PERIOD, row - PERIOD, row).astype(f32)
-        orbit_cos[at, :], orbit_sin[at, :] = cos_sin(row * (1.0 / PERIOD))
-        return carry
-
-    lax.fori_loop(0, ZROWS // 64, orbit_rows, 0)
 
     def factors(s):
         remote(tid_ref, idbuf.at[s], i_send.at[s], i_recv.at[s], owner(s)).wait_recv()
@@ -228,9 +228,8 @@
     def pair_rows(turns, n, carry):
         b, part = n // 2, n % 2
         r0 = pl.multiple_of(b * 16, 16)
-        real = lax.broadcasted_iota(jnp.int32, (16, LANES), 0) + r0 < PERIOD
         lags = [lag_ref[6 * part + q] for q in range(6)]
-        sums = [[jnp.zeros((16, LANES), f32)] * 2 for _ in range(6)]
+        sums = [None] * 6
         for m in range(turns):
             here = pl.ds(r0 + PERIOD * m, 16)
             a, bb = xre[here, :], xim[here, :]
@@ -238,24 +237,28 @@
                 far = pl.ds(r0 + PERIOD * m + lags[q], 16)
                 w = wl[6 * part + q, here, :]
                 c, d = xre[far, :] * w, xim[far, :] * w
-                sums[q] = [sums[q][0] + (a * c + bb * d), sums[q][1] + (a * d - bb * c)]
+                new = [a * c + bb * d, a * d - bb * c]
+                sums[q] = new if m == 0 else [v + w_ for v, w_ in zip(sums[q], new)]
         for q in range(6):
             out = pl.multiple_of((6 * part + q) * (2 * FOLD) + r0, 16)
-            pairs[pl.ds(out, 16), :] = jnp.where(real, sums[q][0], 0.0)
-            pairs[pl.ds(out + FOLD, 16), :] = jnp.where(real, sums[q][1], 0.0)
+            pairs[pl.ds(out, 16), :] = sums[q][0].astype(bf16)
+            pairs[pl.ds(out + FOLD, 16), :] = sums[q][1].astype(bf16)
         return carry
 
     last = (NSFT - PERIOD * (TURNS - 1) + 15) // 16
     lax.fori_loop(0, last * 2, functools.partial(pair_rows, TURNS), 0)
     lax.fori_loop(last * 2, 18 * 2, functools.partial(pair_rows, TURNS - 1), 0)
 
+    for l in range(2 * NLAG):
+        pairs[l * FOLD + PERIOD:(l + 1) * FOLD, :] = jnp.zeros((FOLD - PERIOD, LANES), bf16)
+
     def turn(b, carry):
-        for q in range(6):
-            at = pl.ds(pl.multiple_of((b * 6 + q) * LANES, LANES), LANES)
-            pairs_t[b * 6 + q] = pairs[at, :].T.astype(bf16)
-        return carry
-
-    lax.fori_loop(0, DEPTH // LANES // 6, turn, 0)
+        for q in range(9):
+            at = pl.ds(pl.multiple_of((b * 9 + q) * LANES, LANES), LANES)
+            pairs_t[b * 9 + q] = pairs[at, :].T
+        return carry
+
+    lax.fori_loop(0, DEPTH // LANES // 9, turn, 0)
 
     scale = 1.0 / math.sqrt(NSFT * NLAG)
 
@@ -319,7 +322,7 @@
             pltpu.VMEM((8, ZROWS, LANES), f32),
             pltpu.VMEM((8, ZROWS, LANES), f32),
             pltpu.VMEM((8, DEPTH, LANES), bf16),
-            pltpu.VMEM((DEPTH, LANES), f32),
+            pltpu.VMEM((DEPTH, LANES), bf16),
             pltpu.VMEM((DEPTH // LANES, LANES, LANES), bf16),
             dma((5,)), dma((4,)), dma((4,)), dma((8,)), dma((8,)), dma((16,)), dma((TM,)), dma((16,)), dma((TM,)),
             dma((16,)), dma((16,)), dma((8,)), dma((8,)),

time: 33.8 us -> 33.4 us (0.988)
    pallas_call x1, Pallas kernels: 32.8 us -> 32.5 us  [shards(): pl.pallas_call(kernel, out_shape=pltpu.VMEM((LANES, 8 * LANES), bf16), in...]
where the time goes in v9:
time: 33.4 us; the launch traced here: 33.3 us
  Pallas kernels  32.5 us (97%)
  other arithmetic  0.84 us (3%)
    pallas_call x1, Pallas kernels, shards(): pl.pallas_call(kernel, out_shape=pltpu.VMEM((LANES, 8 * LANES), bf16), in...  32.5 us
    convert_element_type x1, other arithmetic, shards(): return out.astype(f32)  0.84 us

profile of v9, /device:TPU:1, one launch (start us, length us, event | category | flops | bytes accessed | tf_op | source)
XLA Modules:
  0.0 33.3 jit_solution(14987860567119814773)
XLA Ops:
  0.0 32.5 %shard_map.55 = bf16[128,1024]{1,0:T(8,128)(2,1)S(1)} custom-call(f32[768,128]{1,0:T(8,128)} %bitcast.7, s32[12,128]{1,0:T(8,128)} %bitcast.8, s32[2,128]{1,0:T(2,128)} %bitcast.9, f32[3,3]{1,0:T(4,128)} %inter_hbm.1, s32[12]{0:T(128)} %lag_hbm.1), custom_call_target="tpu_custom_call" | custom-call | tf_op jit(solution)/shard_map/pallas_call | solution.py:295
  32.5 0.8 %convert_element_type.3 = f32[128,1024]{1,0:T(8,128)} convert(bf16[128,1024]{1,0:T(8,128)(2,1)S(1)} %shard_map.55) | non-fusion elementwise | flops 131072 | bytes 786432 | tf_op jit(solution)/shard_map/convert_element_type | solution.py:333

commit v10 on v9

--- a/solution.py
+++ b/solution.py
@@ -253,12 +253,12 @@
         pairs[l * FOLD + PERIOD:(l + 1) * FOLD, :] = jnp.zeros((FOLD - PERIOD, LANES), bf16)
 
     def turn(b, carry):
-        for q in range(9):
-            at = pl.ds(pl.multiple_of((b * 9 + q) * LANES, LANES), LANES)
-            pairs_t[b * 9 + q] = pairs[at, :].T
-        return carry
-
-    lax.fori_loop(0, DEPTH // LANES // 9, turn, 0)
+        for q in range(18):
+            at = pl.ds(pl.multiple_of((b * 18 + q) * LANES, LANES), LANES)
+            pairs_t[b * 18 + q] = pairs[at, :].T
+        return carry
+
+    lax.fori_loop(0, DEPTH // LANES // 18, turn, 0)
 
     scale = 1.0 / math.sqrt(NSFT * NLAG)
 

time: 33.4 us -> 33.2 us (level)
  no operation moved by 1% of the time
where the time goes in v10:
time: 33.2 us; the launch traced here: 33 us
  Pallas kernels  32.2 us (97%)
  other arithmetic  0.84 us (3%)
    pallas_call x1, Pallas kernels, shards(): pl.pallas_call(kernel, out_shape=pltpu.VMEM((LANES, 8 * LANES), bf16), in...  32.2 us
    convert_element_type x1, other arithmetic, shards(): return out.astype(f32)  0.84 us

profile of v10, /device:TPU:1, one launch (start us, length us, event | category | flops | bytes accessed | tf_op | source)
XLA Modules:
  0.0 33.0 jit_solution(11325178160803066995)
XLA Ops:
  0.0 32.2 %shard_map.55 = bf16[128,1024]{1,0:T(8,128)(2,1)S(1)} custom-call(f32[768,128]{1,0:T(8,128)} %bitcast.7, s32[12,128]{1,0:T(8,128)} %bitcast.8, s32[2,128]{1,0:T(2,128)} %bitcast.9, f32[3,3]{1,0:T(4,128)} %inter_hbm.1, s32[12]{0:T(128)} %lag_hbm.1), custom_call_target="tpu_custom_call" | custom-call | tf_op jit(solution)/shard_map/pallas_call | solution.py:295
  32.2 0.8 %convert_element_type.3 = f32[128,1024]{1,0:T(8,128)} convert(bf16[128,1024]{1,0:T(8,128)(2,1)S(1)} %shard_map.55) | non-fusion elementwise | flops 131072 | bytes 786432 | tf_op jit(solution)/shard_map/convert_element_type | solution.py:333

commit v11 on v10

--- a/solution.py
+++ b/solution.py
@@ -21,7 +21,7 @@
 TURNS = 6
 LANES = 128
 ROWS = 1600
-ZROWS = 320
+ZROWS = 304
 DEPTH = 2 * NLAG * FOLD
 PART = 1024
 WIDE = 256
@@ -34,7 +34,7 @@
 
 
 def cos_sin(turns):
-    u = turns - jnp.floor(turns + 0.5)
+    u = turns - jnp.round(turns)
     t = u * u
     c = jnp.full_like(t, COS[-1])
     for k in COS[-2::-1]:
@@ -47,7 +47,7 @@
 
 def kernel(x_hbm, det_hbm, tid_hbm, inter_hbm, lag_hbm, o_ref,
            x_ref, det_ref, tid_ref, inter_ref, lag_ref, pbuf, gsend, gbuf, idbuf, send_buf, xrecv, osend, orecv,
-           xre, xim, det, wl, amp_cos, amp_sin, orbit_cos, orbit_sin, zc, zs, fac, pairs, pairs_t,
+           xre, xim, det, wl, amp_cos, amp_sin, orbit_cos, orbit_sin, zc, zs, fac, pairs, pairs_t, scales,
            l_sem, p_send, p_recv, i_send, i_recv, g_send, g_recv, c_send, c_recv, fg_send, f_send, o_send, o_recv):
     tm = lax.axis_index("tm")
     h = lax.axis_index("freq")
@@ -135,13 +135,13 @@
     xim[NSFT:, :] = jnp.zeros((ROWS - NSFT, LANES), f32)
 
     def orbit_rows(b, carry):
-        at = pl.ds(pl.multiple_of(b * 64, 64), 64)
-        row = lax.broadcasted_iota(jnp.int32, (64, LANES), 0) + b * 64
+        at = pl.ds(pl.multiple_of(b * 152, 8), 152)
+        row = lax.broadcasted_iota(jnp.int32, (152, LANES), 0) + b * 152
         row = jnp.where(row >= PERIOD, row - PERIOD, row).astype(f32)
         orbit_cos[at, :], orbit_sin[at, :] = cos_sin(row * (1.0 / PERIOD))
         return carry
 
-    lax.fori_loop(0, ZROWS // 64, orbit_rows, 0)
+    lax.fori_loop(0, ZROWS // 152, orbit_rows, 0)
 
     tid_in.wait()
 
@@ -178,12 +178,12 @@
         amp_sin[...] = jnp.broadcast_to(amp * sq_, (8, LANES))
 
         def z_rows(b, carry):
-            at = pl.ds(pl.multiple_of(b * 64, 64), 64)
+            at = pl.ds(pl.multiple_of(b * 152, 8), 152)
             turns = orbit_sin[at, :] * amp_cos[0:1, :] + orbit_cos[at, :] * amp_sin[0:1, :]
             zc[s, at, :], zs[s, at, :] = cos_sin(turns)
             return carry
 
-        lax.fori_loop(0, ZROWS // 64, z_rows, 0)
+        lax.fori_loop(0, ZROWS // 152, z_rows, 0)
 
         def factor_rows(b, carry):
             r0 = pl.multiple_of(b * 32, 32)
@@ -213,17 +213,22 @@
         forwards[-2].start()
     factors(1)
 
-    for s in range(16):
-        slot = source(s)[0] + 1 - 2 * core
+    def unpack(slots):
+        for s, slot in enumerate(slots):
+            scales[s:s + 1, :] = gbuf[slot]
+        columns = jnp.concatenate([scales[...], jnp.zeros((LANES - 16, LANES), f32)], 0).T[0:SPAN]
+        for s, slot in enumerate(slots):
+            g = jnp.broadcast_to(columns[:, s:s + 1], (SPAN, LANES))
+            at = pl.ds(pl.multiple_of(slot * SPAN, 16), SPAN)
+            xre[at, :] = xrecv[slot, 0:SPAN, :].astype(f32) * g
+            xim[at, :] = xrecv[slot, SPAN:, :].astype(f32) * g
+
+    unpack([source(s)[0] for s in range(16)])
+    there = [source(s)[0] + 1 - 2 * core for s in range(16)]
+    for s, slot in enumerate(there):
         remote(xrecv.at[slot], xrecv.at[slot], f_send.at[s], c_recv.at[slot], other).wait_recv()
         remote(gbuf.at[slot], gbuf.at[slot], fg_send.at[s], g_recv.at[slot], other).wait_recv()
-
-    scales = gbuf[:, 0, :]
-    scales = jnp.concatenate([scales, jnp.zeros((LANES - TM, LANES), f32)], 0).T[0:SPAN]
-    for b in range(TM):
-        g = jnp.broadcast_to(scales[:, b:b + 1], (SPAN, LANES))
-        xre[b * SPAN:(b + 1) * SPAN, :] = xrecv[b, 0:SPAN, :].astype(f32) * g
-        xim[b * SPAN:(b + 1) * SPAN, :] = xrecv[b, SPAN:, :].astype(f32) * g
+    unpack(there)
 
     def pair_rows(turns, n, carry):
         b, part = n // 2, n % 2
@@ -324,6 +329,7 @@
             pltpu.VMEM((8, DEPTH, LANES), bf16),
             pltpu.VMEM((DEPTH, LANES), bf16),
             pltpu.VMEM((DEPTH // LANES, LANES, LANES), bf16),
+            pltpu.VMEM((16, LANES), f32),
             dma((5,)), dma((4,)), dma((4,)), dma((8,)), dma((8,)), dma((16,)), dma((TM,)), dma((16,)), dma((TM,)),
             dma((16,)), dma((16,)), dma((8,)), dma((8,)),
         ],

time: 33.2 us -> 33.1 us (level)
  no operation moved by 1% of the time
where the time goes in v11:
time: 33.1 us; the launch traced here: 33 us
  Pallas kernels  32.1 us (97%)
  other arithmetic  0.84 us (3%)
    pallas_call x1, Pallas kernels, shards(): pl.pallas_call(kernel, out_shape=pltpu.VMEM((LANES, 8 * LANES), bf16), in...  32.1 us
    convert_element_type x1, other arithmetic, shards(): return out.astype(f32)  0.84 us

profile of v11, /device:TPU:1, one launch (start us, length us, event | category | flops | bytes accessed | tf_op | source)
XLA Modules:
  0.0 33.0 jit_solution(16143745080665296822)
XLA Ops:
  0.0 32.1 %shard_map.55 = bf16[128,1024]{1,0:T(8,128)(2,1)S(1)} custom-call(f32[768,128]{1,0:T(8,128)} %bitcast.7, s32[12,128]{1,0:T(8,128)} %bitcast.8, s32[2,128]{1,0:T(2,128)} %bitcast.9, f32[3,3]{1,0:T(4,128)} %inter_hbm.1, s32[12]{0:T(128)} %lag_hbm.1), custom_call_target="tpu_custom_call" | custom-call | tf_op jit(solution)/shard_map/pallas_call | solution.py:300
  32.1 0.8 %convert_element_type.3 = f32[128,1024]{1,0:T(8,128)} convert(bf16[128,1024]{1,0:T(8,128)(2,1)S(1)} %shard_map.55) | non-fusion elementwise | flops 131072 | bytes 786432 | tf_op jit(solution)/shard_map/convert_element_type | solution.py:339

commit v12 on v10

--- a/solution.py
+++ b/solution.py
@@ -265,7 +265,7 @@
     def multiply(n, carry):
         b = n
         lhs = jnp.concatenate([pairs_t[k] for k in range(DEPTH // LANES)], 1)
-        rhs = jnp.concatenate([fac[2 * b], fac[2 * b + 1]], 1)
+        rhs = jnp.concatenate([fac[2 * b, 0:DEPTH, :], fac[2 * b + 1, 0:DEPTH, :]], 1)
         stat = jnp.dot(lhs, rhs, preferred_element_type=f32) * scale
         for q in range(2):
             s = 2 * b + q
@@ -321,7 +321,7 @@
             pltpu.VMEM((ZROWS, LANES), f32),
             pltpu.VMEM((8, ZROWS, LANES), f32),
             pltpu.VMEM((8, ZROWS, LANES), f32),
-            pltpu.VMEM((8, DEPTH, LANES), bf16),
+            pltpu.VMEM((8, DEPTH + 16, LANES), bf16),
             pltpu.VMEM((DEPTH, LANES), bf16),
             pltpu.VMEM((DEPTH // LANES, LANES, LANES), bf16),
             dma((5,)), dma((4,)), dma((4,)), dma((8,)), dma((8,)), dma((16,)), dma((TM,)), dma((16,)), dma((TM,)),

time: 33.2 us -> 33.2 us (level)
  no operation moved by 1% of the time
where the time goes in v12:
time: 33.2 us; the launch traced here: 33 us
  Pallas kernels  32.2 us (97%)
  other arithmetic  0.84 us (3%)
    pallas_call x1, Pallas kernels, shards(): pl.pallas_call(kernel, out_shape=pltpu.VMEM((LANES, 8 * LANES), bf16), in...  32.2 us
    convert_element_type x1, other arithmetic, shards(): return out.astype(f32)  0.84 us

profile of v12, /device:TPU:1, one launch (start us, length us, event | category | flops | bytes accessed | tf_op | source)
XLA Modules:
  0.0 33.0 jit_solution(11074030660729000737)
XLA Ops:
  0.0 32.2 %shard_map.55 = bf16[128,1024]{1,0:T(8,128)(2,1)S(1)} custom-call(f32[768,128]{1,0:T(8,128)} %bitcast.7, s32[12,128]{1,0:T(8,128)} %bitcast.8, s32[2,128]{1,0:T(2,128)} %bitcast.9, f32[3,3]{1,0:T(4,128)} %inter_hbm.1, s32[12]{0:T(128)} %lag_hbm.1), custom_call_target="tpu_custom_call" | custom-call | tf_op jit(solution)/shard_map/pallas_call | solution.py:295
  32.2 0.8 %convert_element_type.3 = f32[128,1024]{1,0:T(8,128)} convert(bf16[128,1024]{1,0:T(8,128)(2,1)S(1)} %shard_map.55) | non-fusion elementwise | flops 131072 | bytes 786432 | tf_op jit(solution)/shard_map/convert_element_type | solution.py:333
